TPU v7x, 32 devices: a whole 2x2x4 slice. The times are simulated.
32 devices in a mesh: gx: 4 (over x, core), gy: 4 (over z), gz: 2 (over y).
Axes of the slice: x: 2, y: 2, z: 4, core: 2. Of those that a mesh axis runs over, the one named last changes fastest.
Arguments:
- field: float32 [64, 1024, 256], P('gx', 'gy', 'gz'), may hold values from -6 to 6
- source: float32 [64, 1024, 256], P('gx', 'gy', 'gz'), may hold values from -6 to 6
Outputs:
- smoothed: float32 [64, 1024, 256], P('gx', 'gy', 'gz')
All inputs are finite; a program needn't handle non-finite values.
Results may differ from a plain program's by a relative error of at most 0.00002.
Values sent between devices are 32-bit elements; how exact they have to be, the bound alone decides.
A program may use at most 64 MiB of HBM per device.

v0:
```python
import functools

import jax
import jax.numpy as jnp
from jax import lax
from jax.experimental import pallas as pl
from jax.experimental.pallas import tpu as pltpu
from jax.sharding import PartitionSpec as P

SWEEPS = 3
MESH = pl.DeviceIdType.MESH
GROUP = 32
PAD = 8
X_LO, X_HI, Y_LO, Y_HI, Z_LO, Z_HI = range(6)


def kernel(sizes, f_hbm, s_hbm, ov, fv, sv, x, src, comb, kb, kr, jb, jr, ib, ir, send, recv, fsem, ssem):
    ngx, ngy, ngz = sizes
    planes, rows, cols = f_hbm.shape
    nm = planes // 2
    half = rows // 2
    per_plane = rows // 8
    rounds = 2 * SWEEPS
    gx, gy, gz = (lax.axis_index(a) for a in ("gx", "gy", "gz"))
    has_lo, has_hi = gx > 0, gx < ngx - 1
    one_z = ngz == 2
    y_lo, y_hi = lax.rem(gy + ngy - 1, ngy), lax.rem(gy + 1, ngy)
    z_lo, z_hi = lax.rem(gz + ngz - 1, ngz), lax.rem(gz + 1, ngz)
    order = [m for a in range(nm // 2) for m in (a, nm - 1 - a)]

    def load(ref, to, sem, m):
        return pltpu.make_async_copy(ref.at[pl.ds(2 * m, 2)], to.at[pl.ds(2 * m, 2)], sem.at[m])

    for m in order:
        load(f_hbm, fv, fsem, m).start()
    for m in order:
        load(s_hbm, sv, ssem, m).start()

    barrier = pltpu.get_barrier_semaphore()

    def greet(device):
        pl.semaphore_signal(barrier, inc=1, device_id=device, device_id_type=MESH)

    @pl.when(has_lo)
    def _():
        greet({"gx": gx - 1})

    @pl.when(has_hi)
    def _():
        greet({"gx": gx + 1})

    ys = [y_lo] if ngy == 2 else [y_lo, y_hi]
    zs = [z_lo] if one_z else [z_lo, z_hi]
    for y in ys:
        greet({"gy": y})
    for z in zs:
        greet({"gz": z})

    row8 = lax.broadcasted_iota(jnp.int32, (8, cols), 0)
    lane = lax.broadcasted_iota(jnp.int32, (8, cols), 1)
    odd8 = lax.rem(row8 + lane, 2)
    pair8 = lax.div(lane, 2)
    odd3 = jnp.broadcast_to(odd8[None], (GROUP, 8, cols)) == 1
    first3 = jnp.broadcast_to(lane[None], (GROUP, 8, cols)) == 0
    last3 = jnp.broadcast_to(lane[None], (GROUP, 8, cols)) == cols - 1
    even_lane = lax.rem(lane, 2) == 0
    odd_lane_half = lax.rem(lax.broadcasted_iota(jnp.int32, (half, cols), 1), 2) == 1

    zero = jnp.zeros((rows, cols), jnp.float32)

    @pl.when(jnp.logical_not(has_lo))
    def _():
        for c in range(2):
            x[c, 0, pl.ds(PAD, rows), :] = zero

    @pl.when(jnp.logical_not(has_hi))
    def _():
        for c in range(2):
            x[c, nm + 1, pl.ds(PAD, rows), :] = zero

    def three(v):
        return v.reshape(GROUP, 8, cols)

    def flat(v):
        return v.reshape(GROUP * 8, cols)

    def pair(produce, store, a, pack_to):
        accs = []
        for h, m in enumerate((a, nm - 1 - a)):
            for blk in range(per_plane // GROUP):
                start = blk * GROUP * 8
                y = produce(a, m, h * per_plane + blk * GROUP, start)
                store(m, start, y)
                if pack_to is not None:
                    acc = jnp.zeros((8, cols), jnp.float32)
                    for g in range(GROUP):
                        q = h * per_plane + blk * GROUP + g
                        acc = jnp.where(pair8 == q, pltpu.roll(y[g], (2 * q + 1) % cols, 1), acc)
                    accs.append(acc)
        if pack_to is not None:
            while len(accs) > 1:
                accs = [p + q for p, q in zip(accs[::2], accs[1::2])]
            pack_to[a] = accs[0]

    def copy(src_ref, dst_ref, to, at, out_dir, in_dir):
        return pltpu.make_async_remote_copy(
            src_ref=src_ref, dst_ref=dst_ref, send_sem=send.at[(out_dir, *at)], recv_sem=recv.at[(in_dir, *at)],
            device_id=to, device_id_type=MESH,
        )

    def x_lo_copy(t):
        return copy(ib.at[0, t], ir.at[1, t], {"gx": gx - 1}, (t, 0), X_LO, X_HI)

    def x_hi_copy(t):
        return copy(ib.at[1, t], ir.at[0, t], {"gx": gx + 1}, (t, 0), X_HI, X_LO)

    def y_copies(t, a):
        return (
            copy(jb.at[0, t, a], jr.at[1, t, a], {"gy": y_lo}, (t, a), Y_LO, Y_HI),
            copy(jb.at[1, t, a], jr.at[0, t, a], {"gy": y_hi}, (t, a), Y_HI, Y_LO),
        )

    def z_copies(t, a):
        up = copy(kb.at[t, a], kr.at[0, t, a], {"gz": z_hi}, (t, a), Z_HI, Z_LO)
        if one_z:
            return (up,)
        return (up, copy(kb.at[t, a], kr.at[1, t, a], {"gz": z_lo}, (t, a), Z_LO, Z_HI))

    def face(c, side):
        m = 1 if side == 0 else nm
        even = x[c, m, pl.ds(PAD, half, stride=2), :]
        odd = x[c, m, pl.ds(PAD + 1, half, stride=2), :]
        wanted = c if side == 0 else 1 - c
        return jnp.where(odd_lane_half, even, odd) if wanted == 1 else jnp.where(odd_lane_half, odd, even)

    def send_x(c, t):
        @pl.when(has_lo)
        def _():
            ib[0, t] = face(c, 0)
            x_lo_copy(t).start()

        @pl.when(has_hi)
        def _():
            ib[1, t] = face(c, 1)
            x_hi_copy(t).start()

    def send_z(t, a):
        for z in z_copies(t, a):
            z.start()

    def send_y(t, a, outermost):
        for h, m in enumerate((a, nm - 1 - a)):
            low, high = outermost(a, m, h)
            jb[0, t, a, pl.ds(h, 1), :] = low
            jb[1, t, a, pl.ds(h, 1), :] = high
        for y in y_copies(t, a):
            y.start()

    def take_yz(c, t, a):
        for z in z_copies(t, a):
            z.wait_recv()
        low = kr[0, t, a]
        high = low if one_z else kr[1, t, a]
        comb[a] = jnp.where(even_lane, pltpu.roll(high, cols - 1, 1), pltpu.roll(low, 1, 1))
        for y in y_copies(t, a):
            y.wait_recv()
        for h, m in enumerate((a, nm - 1 - a)):
            x[c, m + 1, pl.ds(PAD - 1, 1), :] = jr[0, t, a, pl.ds(h, 1), :]
            x[c, m + 1, pl.ds(PAD + rows, 1), :] = jr[1, t, a, pl.ds(h, 1), :]

    def take_x(c, t):
        @pl.when(has_lo)
        def _():
            x_hi_copy_in = copy(ib.at[1, t], ir.at[0, t], {"gx": gx - 1}, (t, 0), X_HI, X_LO)
            x_hi_copy_in.wait_recv()
            got = ir[0, t]
            x[c, 0, pl.ds(PAD, half, stride=2), :] = got
            x[c, 0, pl.ds(PAD + 1, half, stride=2), :] = got

        @pl.when(has_hi)
        def _():
            x_lo_copy_in = copy(ib.at[0, t], ir.at[1, t], {"gx": gx + 1}, (t, 0), X_LO, X_HI)
            x_lo_copy_in.wait_recv()
            got = ir[1, t]
            x[c, nm + 1, pl.ds(PAD, half, stride=2), :] = got
            x[c, nm + 1, pl.ds(PAD + 1, half, stride=2), :] = got

    def store_to(c):
        def store(m, start, y):
            x[c, m + 1, pl.ds(PAD + start, GROUP * 8), :] = flat(y)

        return store

    def black_of_field(a, m, q0, start):
        low = three(fv[2 * m, pl.ds(start, GROUP * 8), :])
        high = three(fv[2 * m + 1, pl.ds(start, GROUP * 8), :])
        return jnp.where(odd3, low, high)

    def pack_field(a, carry):
        for m in (a, nm - 1 - a):
            load(f_hbm, fv, fsem, m).wait()
        pair(black_of_field, store_to(1), a, kb.at[0])
        return carry

    def split_source(m, carry):
        for blk in range(per_plane // GROUP):
            rs = pl.ds(blk * GROUP * 8, GROUP * 8)
            low, high = three(sv[2 * m, rs, :]), three(sv[2 * m + 1, rs, :])
            src[0, m, rs, :] = flat(jnp.where(odd3, high, low))
            src[1, m, rs, :] = flat(jnp.where(odd3, low, high))
        return carry

    def split_pair(a, carry):
        for m in (a, nm - 1 - a):
            load(s_hbm, sv, ssem, m).wait()
            split_source(m, 0)
        return carry

    lax.fori_loop(0, nm // 2, pack_field, 0)
    lax.fori_loop(0, nm // 2, split_pair, 0)
    pl.semaphore_wait(barrier, len(ys) + len(zs) + has_lo.astype(jnp.int32) + has_hi.astype(jnp.int32))
    send_x(1, 0)

    def stored_rows(a, m, h):
        return x[1, m + 1, pl.ds(PAD, 1), :], x[1, m + 1, pl.ds(PAD + rows - 1, 1), :]

    for a in range(nm // 2):
        send_y(0, a, stored_rows)
        send_z(0, a)

    def relax(c, t):
        d = 1 - c

        def produce(a, m, q0, start):
            rs = pl.ds(PAD + start, GROUP * 8)
            here = three(x[d, m + 1, rs, :])
            below, above = three(x[d, m, rs, :]), three(x[d, m + 2, rs, :])
            beside = jnp.where(odd3, above, below) if c == 0 else jnp.where(odd3, below, above)
            total = three(src[c, m, pl.ds(start, GROUP * 8), :]) + here + beside
            total = total + three(x[d, m + 1, pl.ds(PAD + start - 1, GROUP * 8), :])
            total = total + three(x[d, m + 1, pl.ds(PAD + start + 1, GROUP * 8), :])
            edges = comb[a]
            edge = jnp.stack(
                [pltpu.roll(edges, (2 * cols - (2 * (q0 + g) + 1)) % cols, 1) for g in range(GROUP)], axis=0
            )
            total = total + jnp.where(first3, edge, pltpu.roll(here, 1, 2))
            total = total + jnp.where(last3, edge, pltpu.roll(here, cols - 1, 2))
            return total * jnp.float32(1.0 / 6.0)

        return produce

    def early_rows(c):
        d = 1 - c

        def tile(a, m, q, start):
            rs = pl.ds(PAD + start, 8)
            here = x[d, m + 1, rs, :]
            below, above = x[d, m, rs, :], x[d, m + 2, rs, :]
            beside = jnp.where(odd8 == 1, above, below) if c == 0 else jnp.where(odd8 == 1, below, above)
            total = src[c, m, pl.ds(start, 8), :] + here + beside
            total = total + x[d, m + 1, pl.ds(PAD + start - 1, 8), :]
            total = total + x[d, m + 1, pl.ds(PAD + start + 1, 8), :]
            edge = pltpu.roll(comb[a], (2 * cols - (2 * q + 1)) % cols, 1)
            total = total + jnp.where(lane == 0, edge, pltpu.roll(here, 1, 1))
            total = total + jnp.where(lane == cols - 1, edge, pltpu.roll(here, cols - 1, 1))
            return total * jnp.float32(1.0 / 6.0)

        def outermost(a, m, h):
            q = h * per_plane
            return tile(a, m, q, 0)[0:1], tile(a, m, q + per_plane - 1, rows - 8)[7:8]

        return outermost

    def store_out(m, start, y):
        red = three(x[0, m + 1, pl.ds(PAD + start, GROUP * 8), :])
        rs = pl.ds(start, GROUP * 8)
        ov[2 * m, rs, :] = flat(jnp.where(odd3, y, red))
        ov[2 * m + 1, rs, :] = flat(jnp.where(odd3, red, y))

    for t in range(rounds):
        c = t % 2
        final = t == rounds - 1
        store = store_out if final else store_to(c)
        pack = None if final else kb.at[t + 1]

        def piece(a, first=False):
            take_yz(1 - c, t, a)
            if first:
                take_x(1 - c, t)
            if not final:
                send_y(t + 1, a, early_rows(c))
            pair(relax(c, t), store, a, pack)
            if not final:
                if first:
                    send_x(c, t + 1)
                send_z(t + 1, a)

        def body(a, carry):
            piece(a)
            return carry

        piece(0, True)
        lax.fori_loop(1, nm // 2, body, 0)

    for t in range(rounds):
        for a in range(nm // 2):
            for cp in z_copies(t, a) + y_copies(t, a):
                cp.wait_send()

        @pl.when(has_lo)
        def _():
            x_lo_copy(t).wait_send()

        @pl.when(has_hi)
        def _():
            x_hi_copy(t).wait_send()


def solution(mesh):
    sizes = tuple(mesh.shape[a] for a in ("gx", "gy", "gz"))

    def on_device(field, source):
        planes, rows, cols = field.shape
        nm, rounds = planes // 2, 2 * SWEEPS
        assert planes % 4 == 0 and rows % (8 * GROUP) == 0 and cols == 128 and rows // 2 == cols
        f32 = jnp.float32
        return pl.pallas_call(
            functools.partial(kernel, sizes),
            out_shape=jax.ShapeDtypeStruct(field.shape, f32),
            in_specs=[pl.BlockSpec(memory_space=pltpu.HBM)] * 2,
            out_specs=pl.BlockSpec(memory_space=pltpu.VMEM),
            scratch_shapes=[
                pltpu.VMEM(field.shape, f32),
                pltpu.VMEM(field.shape, f32),
                pltpu.VMEM((2, nm + 2, rows + 2 * PAD, cols), f32),
                pltpu.VMEM((2, nm, rows, cols), f32),
                pltpu.VMEM((nm // 2, 8, cols), f32),
                pltpu.VMEM((rounds, nm // 2, 8, cols), f32),
                pltpu.VMEM((2, rounds, nm // 2, 8, cols), f32),
                pltpu.VMEM((2, rounds, nm // 2, 2, cols), f32),
                pltpu.VMEM((2, rounds, nm // 2, 2, cols), f32),
                pltpu.VMEM((2, rounds, rows // 2, cols), f32),
                pltpu.VMEM((2, rounds, rows // 2, cols), f32),
                pltpu.SemaphoreType.DMA((6, rounds, nm // 2)),
                pltpu.SemaphoreType.DMA((6, rounds, nm // 2)),
                pltpu.SemaphoreType.DMA((nm,)),
                pltpu.SemaphoreType.DMA((nm,)),
            ],
            compiler_params=pltpu.CompilerParams(
                collective_id=0, has_side_effects=True, vmem_limit_bytes=50 * 1024 * 1024
            ),
        )(field, source)

    spec = P("gx", "gy", "gz")
    return jax.shard_map(on_device, mesh=mesh, in_specs=(spec, spec), out_specs=spec, check_vma=False)
```

profile of v0, /device:TPU:1, one launch (start us, length us, event | category | flops | bytes accessed | tf_op | source)
XLA Modules:
  0.0 32.8 jit_solution(8849381412353959836)
XLA Ops:
  0.0 31.5 %shard_map.28 = f32[16,256,128]{2,1,0:T(8,128)S(1)} custom-call(f32[16,256,128]{2,1,0:T(8,128)} %f_hbm.1, f32[16,256,128]{2,1,0:T(8,128)} %s_hbm.1), custom_call_target="tpu_custom_call" | custom-call | tf_op jit(solution)/shard_map/pallas_call | solution.py:327
  31.5 1.3 %copy.4 = f32[16,256,128]{2,1,0:T(8,128)} copy(f32[16,256,128]{2,1,0:T(8,128)S(1)} %shard_map.28) | data formatting | bytes 4194304
where the time goes:
time: 33.4 us; the launch traced here: 32.8 us
  Pallas kernels  31.5 us (94%)
  local copies, waits for them, and re-layouts  1.32 us (4%)
    pallas_call x1, Pallas kernels, on_device(): pl.pallas_call(functools.partial(kernel, sizes), out_shape=jax.ShapeDtype...  31.5 us
    unnamed x1, local copies, waits for them, and re-layouts  1.32 us

commit v1 on v0

v1 whole, which is shorter than its diff:
```python
import functools

import jax
import jax.numpy as jnp
from jax import lax
from jax.experimental import pallas as pl
from jax.experimental.pallas import tpu as pltpu
from jax.sharding import PartitionSpec as P

SWEEPS = 3
MESH = pl.DeviceIdType.MESH
PAD = 16
X, Y, Z, XY, YZ, XZ, SX, SY, SZ = 0, 2, 4, 6, 10, 14, 18, 20, 22
SIXTH = 1.0 / 6.0


def kernel(
    sizes, f_hbm, s_hbm, ov, fv, sv, x, src, eb, er, qb, sq, yzb, sqs,
    pk, jb, yzs, sys_, xg, jr, zr, xyr, yzr, xzr, syr, szr, send, recv, fsem, ssem,
):
    ngx, ngy, ngz = sizes
    planes, rows, cols = f_hbm.shape
    nm = planes // 2
    ng = rows // 8
    gx, gy, gz = (lax.axis_index(a) for a in ("gx", "gy", "gz"))
    has = (gx > 0, gx < ngx - 1)
    nz = 1 if ngz == 2 else 2
    y_to = (lax.rem(gy + ngy - 1, ngy), lax.rem(gy + 1, ngy))
    z_to = (lax.rem(gz + 1, ngz), lax.rem(gz + ngz - 1, ngz))[:nz]
    x_to = (gx - 1, gx + 1)
    last = cols - 1

    def load(ref, to, sem, m):
        return pltpu.make_async_copy(ref.at[pl.ds(2 * m, 2)], to.at[pl.ds(2 * m, 2)], sem.at[m])

    order = [m for a in range(nm // 2) for m in (a, nm - 1 - a)]
    for m in order:
        load(f_hbm, fv, fsem, m).start()
    for m in order:
        load(s_hbm, sv, ssem, m).start()

    barrier = pltpu.get_barrier_semaphore()

    def greet(device):
        pl.semaphore_signal(barrier, inc=1, device_id=device, device_id_type=MESH)

    for y in y_to:
        greet({"gy": y})
        for z in z_to:
            greet({"gy": y, "gz": z})
    for z in z_to:
        greet({"gz": z})
    for sx in range(2):

        @pl.when(has[sx])
        def _():
            greet({"gx": x_to[sx]})
            for y in y_to:
                greet({"gx": x_to[sx], "gy": y})
            for z in z_to:
                greet({"gx": x_to[sx], "gz": z})

    sub = lax.broadcasted_iota(jnp.int32, (8, cols), 0)
    lane = lax.broadcasted_iota(jnp.int32, (8, cols), 1)
    odd = lax.rem(sub + lane, 2) == 1
    first, final_lane = lane == 0, lane == last
    quad = lax.div(lane, 4)
    pos = lax.rem(lane, 4)
    pos0, pos1, pos3, low_half = pos == 0, pos == 1, pos == 3, pos < 2
    odd_q = lax.rem(sub + jnp.where(pos1, 1, 0), 2) == 1
    top, bottom = sub == 0, sub == 7
    hi_quad = ng % (cols // 4)
    in_lo, in_hi = quad == cols // 4 - 1, quad == hi_quad
    zero = jnp.zeros((8, cols), jnp.float32)

    def roll(v, by):
        by = by % cols
        return v if by == 0 else pltpu.roll(v, by, 1)

    for sx in range(2):
        m = (0, nm + 1)[sx]

        @pl.when(jnp.logical_not(has[sx]))
        def _():
            for c in range(2):
                x[c, m] = jnp.zeros((rows + 2 * PAD, cols), jnp.float32)
            eb[m] = zero
            qb[m] = zero

    def copy(src_ref, dst_ref, device, slot, t):
        return pltpu.make_async_remote_copy(
            src_ref=src_ref, dst_ref=dst_ref, send_sem=send.at[slot, t], recv_sem=recv.at[slot, t],
            device_id=device, device_id_type=MESH,
        )

    edge_m = (0, nm - 1)

    def msg_x(sx, t):
        return copy(x.at[1, edge_m[sx] + 1, pl.ds(PAD, rows)], xg.at[1 - sx, t], {"gx": x_to[sx]}, X + sx, t)

    def msg_y(sy, t):
        return copy(jb.at[sy, t], jr.at[1 - sy, t], {"gy": y_to[sy]}, Y + sy, t)

    def msg_z(zd, t):
        return copy(pk.at[t], zr.at[zd, t], {"gz": z_to[zd]}, Z + zd, t)

    def msg_xy(sx, sy, t):
        return copy(
            jb.at[sy, t, edge_m[sx]], xyr.at[1 - sx, 1 - sy, t], {"gx": x_to[sx], "gy": y_to[sy]}, XY + 2 * sx + sy, t
        )

    def msg_yz(sy, zd, t):
        return copy(yzs.at[sy, t], yzr.at[1 - sy, zd, t], {"gy": y_to[sy], "gz": z_to[zd]}, YZ + 2 * sy + zd, t)

    def msg_xz(sx, zd, t):
        return copy(
            pk.at[t, edge_m[sx]], xzr.at[1 - sx, zd, t], {"gx": x_to[sx], "gz": z_to[zd]}, XZ + 2 * sx + zd, t
        )

    def msg_sx(sx):
        return copy(
            src.at[0, edge_m[sx] + 1, pl.ds(PAD, rows)], src.at[0, (nm + 1, 0)[sx], pl.ds(PAD, rows)],
            {"gx": x_to[sx]}, SX + sx, 0,
        )

    def msg_sy(sy):
        return copy(sys_.at[sy], syr.at[1 - sy], {"gy": y_to[sy]}, SY + sy, 0)

    def msg_sz(zd):
        return copy(sqs, szr.at[zd], {"gz": z_to[zd]}, SZ + zd, 0)

    def send_far(t):
        for sy in range(2):
            for zd in range(nz):
                msg_yz(sy, zd, t).start()
        for sx in range(2):

            @pl.when(has[sx])
            def _():
                for sy in range(2):
                    msg_xy(sx, sy, t).start()

        for sy in range(2):
            msg_y(sy, t).start()

    def send_x(t):
        for sx in range(2):

            @pl.when(has[sx])
            def _():
                for zd in range(nz):
                    msg_xz(sx, zd, t).start()
                msg_x(sx, t).start()

    def send_z(t):
        for zd in range(nz):
            msg_z(zd, t).start()

    def rows_of(g, shift=0):
        return pl.ds(PAD + 8 * g + shift, 8)

    def keep_rows(t, m, g, y, sy):
        if sy == 0:
            jb[0, t, m] = y[0:2]
            yzs[0, t, pl.ds(m, 1), :] = roll(y, 4 * hi_quad + 2)[0:1]
        else:
            jb[1, t, m] = y[6:8]
            yzs[1, t, pl.ds(m, 1), :] = roll(y, -2)[7:8]

    def packed(acc, g, y):
        return jnp.where(quad == g, roll(y, 4 * g + 2), acc)

    def field_plane(m, carry):
        load(f_hbm, fv, fsem, m).wait()
        acc = [zero] * 4
        for g in range(ng):
            rs = pl.ds(8 * g, 8)
            y = jnp.where(odd, fv[2 * m, rs, :], fv[2 * m + 1, rs, :])
            x[1, m + 1, rows_of(g), :] = y
            acc[g % 4] = packed(acc[g % 4], g, y)
            if g == 0:
                keep_rows(0, m, g, y, 0)
            if g == ng - 1:
                keep_rows(0, m, g, y, 1)
        pk[0, m] = (acc[0] + acc[1]) + (acc[2] + acc[3])
        return carry

    def source_plane(m, carry):
        load(s_hbm, sv, ssem, m).wait()
        acc = [zero] * 4
        for g in range(ng):
            rs = pl.ds(8 * g, 8)
            low, high = sv[2 * m, rs, :], sv[2 * m + 1, rs, :]
            red = jnp.where(odd, high, low)
            src[0, m + 1, rows_of(g), :] = red
            src[1, m + 1, rows_of(g), :] = jnp.where(odd, low, high)
            acc[g % 4] = packed(acc[g % 4], g, red)
            if g == 0:
                sys_[0, pl.ds(m, 1), :] = red[0:1]
            if g == ng - 1:
                sys_[1, pl.ds(m, 1), :] = red[7:8]
        sqs[m] = (acc[0] + acc[1]) + (acc[2] + acc[3])
        return carry

    lax.fori_loop(0, nm, field_plane, 0)
    near = [h.astype(jnp.int32) for h in has]
    pl.semaphore_wait(barrier, 2 + 3 * nz + (near[0] + near[1]) * (3 + nz))
    send_far(0)
    send_x(0)
    send_z(0)
    lax.fori_loop(0, nm, source_plane, 0)
    for sy in range(2):
        msg_sy(sy).start()
    for zd in range(nz):
        msg_sz(zd).start()
    for sx in range(2):

        @pl.when(has[sx])
        def _():
            msg_sx(sx).start()

    def tile(c, m, g, edge, side=None):
        d = 1 - c
        rs = rows_of(g)
        here = x[d, m + 1, rs, :]
        if side is None:
            below, above = x[d, m, rs, :], x[d, m + 2, rs, :]
            beside = jnp.where(odd, above, below) if c == 0 else jnp.where(odd, below, above)
        else:
            beside = x[d, m + 1 + side, rs, :]
        total = (src[c, m + 1, rs, :] + here) + (beside + x[d, m + 1, rows_of(g, -1), :])
        total = total + x[d, m + 1, rows_of(g, 1), :]
        total = total + jnp.where(first, edge, roll(here, 1))
        total = total + jnp.where(final_lane, edge, roll(here, -1))
        return total * jnp.float32(SIXTH)

    def edge_at(v, g):
        return roll(v, -(4 * g + 2))

    def red_plane(m, groups, side=None):
        v = eb[m + 1]
        for g in groups:
            x[0, m + 1, rows_of(g), :] = tile(0, m, g, edge_at(v, g), side)

    def put(m, g, y, final):
        if final:
            red = x[0, m + 1, rows_of(g), :]
            rs = pl.ds(8 * g, 8)
            ov[2 * m, rs, :] = jnp.where(odd, y, red)
            ov[2 * m + 1, rs, :] = jnp.where(odd, red, y)
        else:
            x[1, m + 1, rows_of(g), :] = y

    def black_plane(m, groups, t, final):
        v = er[m]
        acc = [zero] * 4
        for g in groups:
            y = tile(1, m, g, edge_at(v, g))
            put(m, g, y, final)
            if not final:
                acc[g % 4] = packed(acc[g % 4], g, y)
        if not final:
            pk[t + 1, m] = pk[t + 1, m] + ((acc[0] + acc[1]) + (acc[2] + acc[3]))

    inner = range(1, ng - 1)

    def swapped(lo, hi):
        return jnp.where(pos1, roll(hi, -1), roll(lo, 1))

    for t in range(SWEEPS):
        final = t == SWEEPS - 1
        hi_z = nz - 1
        for zd in range(nz):
            msg_z(zd, t).wait_recv()
        for m in range(nm):
            lo, hi = zr[0, t, m], zr[hi_z, t, m]
            qb[m + 1] = jnp.where(low_half, lo, hi)
            eb[m + 1] = swapped(lo, hi)
        if t == 0:
            pass

        def red_inner(m, carry):
            red_plane(m, inner)
            return carry

        lax.fori_loop(1, nm - 1, red_inner, 0)

        for sx in range(2):
            m, at = ((-1, 0), (nm, nm + 1))[sx]

            @pl.when(has[sx])
            def _():
                for zd in range(nz):
                    msg_xz(1 - sx, zd, t).wait_recv()
                lo, hi = xzr[sx, 0, t], xzr[sx, hi_z, t]
                qb[at] = jnp.where(low_half, lo, hi)
                eb[at] = swapped(lo, hi)
                msg_x(1 - sx, t).wait_recv()
                if t == 0:
                    msg_sx(1 - sx).wait_recv()
                x[1, at, pl.ds(PAD, rows), :] = xg[sx, t]
                red_plane(m, inner, (1, -1)[sx])

        for m in edge_m:
            red_plane(m, inner)

        if t == 0:
            for zd in range(nz):
                msg_sz(zd).wait_recv()
            for m in range(nm):
                sq[m] = jnp.where(low_half, szr[0, m], szr[hi_z, m])
            for sy in range(2):
                msg_sy(sy).wait_recv()
                for m in range(nm):
                    src[0, m + 1, pl.ds((PAD + rows, PAD - 1)[sy], 1), :] = syr[1 - sy, pl.ds(m, 1), :]
        for sy in range(2):
            msg_y(sy, t).wait_recv()
            for m in range(nm):
                x[1, m + 1, pl.ds((PAD + rows, PAD - 2)[sy], 2), :] = jr[1 - sy, t, m]
        for sx in range(2):

            @pl.when(has[sx])
            def _():
                for sy in range(2):
                    msg_xy(1 - sx, sy, t).wait_recv()
                    x[1, (0, nm + 1)[sx], pl.ds((PAD + rows, PAD - 2)[sy], 2), :] = xyr[sx, 1 - sy, t]

        low8 = lax.rem(lax.broadcasted_iota(jnp.int32, (nm, cols), 1), 4)
        for sy in range(2):
            for zd in range(nz):
                msg_yz(sy, zd, t).wait_recv()
            lo, hi = yzr[1 - sy, 0, t], yzr[1 - sy, hi_z, t]
            yzb[1 - sy] = jnp.where(low8 < 2, lo, hi)
            yzb[2 + 1 - sy] = jnp.where(low8 == 1, pltpu.roll(hi, last, 1), pltpu.roll(lo, 1, 1))

        def spread(k, m):
            return jnp.broadcast_to(yzb[k, pl.ds(m, 1), :], (8, cols))

        for sx in range(2):
            m = (-1, nm)[sx]

            @pl.when(has[sx])
            def _():
                red_plane(m, (0, ng - 1), (1, -1)[sx])

        for m in range(nm):
            red_plane(m, (0, ng - 1))
            for g, k in ((-1, 2), (ng, 3)):
                x[0, m + 1, rows_of(g), :] = tile(0, m, g, edge_at(spread(k, m), g))
            own, q = pk[t, m], qb[m + 1]
            zsum = roll(jnp.where(pos0, q, own), 1) + roll(jnp.where(pos3, q, own), -1)
            beside = jnp.where(odd_q, qb[m + 2], qb[m])
            up = jnp.where(bottom, roll(jnp.where(in_lo, spread(0, m), q), 4), q)
            down = jnp.where(top, roll(jnp.where(in_hi, spread(1, m), q), -4), q)
            total = (sq[m] + q) + (beside + pltpu.roll(up, 1, 0)) + (pltpu.roll(down, 7, 0) + zsum)
            red = total * jnp.float32(SIXTH)
            er[m] = swapped(red, red)

        if not final:
            for sx in range(2):

                @pl.when(has[sx])
                def _():
                    msg_x(sx, t).wait_send()

        for m in range(nm):
            v = er[m]
            acc = zero
            for sy, g in ((0, 0), (1, ng - 1)):
                y = tile(1, m, g, edge_at(v, g))
                put(m, g, y, final)
                if not final:
                    keep_rows(t + 1, m, g, y, sy)
                    acc = packed(acc, g, y)
            if not final:
                pk[t + 1, m] = acc
        if not final:
            send_far(t + 1)
        for m in edge_m:
            black_plane(m, inner, t, final)
        if not final:
            send_x(t + 1)

        def black_inner(m, carry):
            black_plane(m, inner, t, final)
            return carry

        lax.fori_loop(1, nm - 1, black_inner, 0)
        if not final:
            send_z(t + 1)

    for sy in range(2):
        msg_sy(sy).wait_send()
    for zd in range(nz):
        msg_sz(zd).wait_send()
    for t in range(SWEEPS):
        for sy in range(2):
            msg_y(sy, t).wait_send()
            for zd in range(nz):
                msg_yz(sy, zd, t).wait_send()
        for zd in range(nz):
            msg_z(zd, t).wait_send()
    for sx in range(2):

        @pl.when(has[sx])
        def _():
            msg_sx(sx).wait_send()
            msg_x(sx, SWEEPS - 1).wait_send()
            for t in range(SWEEPS):
                for sy in range(2):
                    msg_xy(sx, sy, t).wait_send()
                for zd in range(nz):
                    msg_xz(sx, zd, t).wait_send()


def solution(mesh):
    sizes = tuple(mesh.shape[a] for a in ("gx", "gy", "gz"))

    def on_device(field, source):
        planes, rows, cols = field.shape
        nm, ng, nz = planes // 2, rows // 8, 1 if sizes[2] == 2 else 2
        assert planes % 4 == 0 and nm >= 4 and rows % 8 == 0 and cols == 128 and 4 * ng <= cols
        f32 = jnp.float32
        vm = lambda *shape: pltpu.VMEM(shape, f32)
        return pl.pallas_call(
            functools.partial(kernel, sizes),
            out_shape=jax.ShapeDtypeStruct(field.shape, f32),
            in_specs=[pl.BlockSpec(memory_space=pltpu.HBM)] * 2,
            out_specs=pl.BlockSpec(memory_space=pltpu.VMEM),
            scratch_shapes=[
                vm(*field.shape),
                vm(*field.shape),
                vm(2, nm + 2, rows + 2 * PAD, cols),
                vm(2, nm + 2, rows + 2 * PAD, cols),
                vm(nm + 2, 8, cols),
                vm(nm, 8, cols),
                vm(nm + 2, 8, cols),
                vm(nm, 8, cols),
                vm(4, nm, cols),
                vm(nm, 8, cols),
                vm(SWEEPS, nm, 8, cols),
                vm(2, SWEEPS, nm, 2, cols),
                vm(2, SWEEPS, nm, cols),
                vm(2, nm, cols),
                vm(2, SWEEPS, rows, cols),
                vm(2, SWEEPS, nm, 2, cols),
                vm(nz, SWEEPS, nm, 8, cols),
                vm(2, 2, SWEEPS, 2, cols),
                vm(2, nz, SWEEPS, nm, cols),
                vm(2, nz, SWEEPS, 8, cols),
                vm(2, nm, cols),
                vm(nz, nm, 8, cols),
                pltpu.SemaphoreType.DMA((24, SWEEPS)),
                pltpu.SemaphoreType.DMA((24, SWEEPS)),
                pltpu.SemaphoreType.DMA((nm,)),
                pltpu.SemaphoreType.DMA((nm,)),
            ],
            compiler_params=pltpu.CompilerParams(
                collective_id=0, has_side_effects=True, vmem_limit_bytes=50 * 1024 * 1024
            ),
        )(field, source)

    spec = P("gx", "gy", "gz")
    return jax.shard_map(on_device, mesh=mesh, in_specs=(spec, spec), out_specs=spec, check_vma=False)
```

time: 33.4 us -> 30.4 us (0.910); the launches traced: 32.8 us -> 30.2 us
  Pallas kernels: 31.5 us -> 28.9 us
    pallas_call x1, Pallas kernels: 31.5 us -> 28.9 us  [on_device(): pl.pallas_call(functools.partial(kernel, sizes), out_shape=jax.ShapeDtype...]
where the time goes in v1:
time: 30.4 us; the launch traced here: 30.2 us
  Pallas kernels  28.9 us (95%)
  local copies, waits for them, and re-layouts  1.32 us (4%)
    pallas_call x1, Pallas kernels, on_device(): pl.pallas_call(functools.partial(kernel, sizes), out_shape=jax.ShapeDtype...  28.9 us
    unnamed x1, local copies, waits for them, and re-layouts  1.32 us

profile of v1, /device:TPU:1, one launch (start us, length us, event | category | flops | bytes accessed | tf_op | source)
XLA Modules:
  0.0 30.2 jit_solution(5394502656655869307)
XLA Ops:
  0.0 28.9 %shard_map.28 = f32[16,256,128]{2,1,0:T(8,128)S(1)} custom-call(f32[16,256,128]{2,1,0:T(8,128)} %f_hbm.1, f32[16,256,128]{2,1,0:T(8,128)} %s_hbm.1), custom_call_target="tpu_custom_call" | custom-call | tf_op jit(solution)/shard_map/pallas_call | solution.py:425
  28.9 1.3 %copy.4 = f32[16,256,128]{2,1,0:T(8,128)} copy(f32[16,256,128]{2,1,0:T(8,128)S(1)} %shard_map.28) | data formatting | bytes 4194304

commit v2 on v1

v2 whole, which is shorter than its diff:
```python
import functools

import jax
import jax.numpy as jnp
from jax import lax
from jax.experimental import pallas as pl
from jax.experimental.pallas import tpu as pltpu
from jax.sharding import PartitionSpec as P

SWEEPS = 3
MESH = pl.DeviceIdType.MESH
PAD = 16
X, Y, Z, XY, YZ, XZ, SX, SY, SZ = 0, 2, 4, 6, 10, 14, 18, 20, 22
SIXTH = 1.0 / 6.0


def kernel(
    sizes, f_hbm, s_hbm, ov, fv, sv, x0, x1, s0, s1, eb, er, qb, sq, yzb, sqs,
    pk, jb, yzs, sys_, xg, jr, zr, xyr, yzr, xzr, syr, szr, send, recv, fsem, ssem,
):
    ngx, ngy, ngz = sizes
    planes, rows, cols = f_hbm.shape
    nm = planes // 2
    ng = rows // 8
    gx, gy, gz = (lax.axis_index(a) for a in ("gx", "gy", "gz"))
    has = (gx > 0, gx < ngx - 1)
    nz = 1 if ngz == 2 else 2
    y_to = (lax.rem(gy + ngy - 1, ngy), lax.rem(gy + 1, ngy))
    z_to = (lax.rem(gz + 1, ngz), lax.rem(gz + ngz - 1, ngz))[:nz]
    x_to = (gx - 1, gx + 1)
    last = cols - 1
    edge_m = (0, nm - 1)

    def load(ref, to, sem, m):
        return pltpu.make_async_copy(ref.at[pl.ds(2 * m, 2)], to.at[pl.ds(2 * m, 2)], sem.at[m])

    def load_ends(sy):
        rs = pl.ds((0, rows - 8)[sy], 8)
        return pltpu.make_async_copy(f_hbm.at[:, rs], fv.at[:, rs], fsem.at[nm + sy])

    def load_field(m):
        at = (pl.ds(2 * m, 2), pl.ds(8, rows - 16))
        return pltpu.make_async_copy(f_hbm.at[at], fv.at[at], fsem.at[m])

    order = [*edge_m, *range(1, nm - 1)]
    for sy in range(2):
        load_ends(sy).start()
    for m in order:
        load_field(m).start()
    for m in order:
        load(s_hbm, sv, ssem, m).start()

    barrier = pltpu.get_barrier_semaphore()

    def greet(device):
        pl.semaphore_signal(barrier, inc=1, device_id=device, device_id_type=MESH)

    for y in y_to:
        greet({"gy": y})
        for z in z_to:
            greet({"gy": y, "gz": z})
    for z in z_to:
        greet({"gz": z})
    for sx in range(2):

        @pl.when(has[sx])
        def _():
            greet({"gx": x_to[sx]})
            for y in y_to:
                greet({"gx": x_to[sx], "gy": y})
            for z in z_to:
                greet({"gx": x_to[sx], "gz": z})

    sub = lax.broadcasted_iota(jnp.int32, (8, cols), 0)
    lane = lax.broadcasted_iota(jnp.int32, (8, cols), 1)
    odd = lax.rem(sub + lane, 2) == 1
    first, final_lane = lane == 0, lane == last
    quad = lax.div(lane, 4)
    pos = lax.rem(lane, 4)
    pos0, pos1, pos3, low_half = pos == 0, pos == 1, pos == 3, pos < 2
    odd_q = lax.rem(sub + jnp.where(pos1, 1, 0), 2) == 1
    top, bottom = sub == 0, sub == 7
    hi_quad = ng % (cols // 4)
    in_lo, in_hi = quad == cols // 4 - 1, quad == hi_quad
    zero = jnp.zeros((8, cols), jnp.float32)

    def roll(v, by):
        by = by % cols
        return v if by == 0 else pltpu.roll(v, by, 1)

    for sx in range(2):
        m = (0, nm + 1)[sx]

        @pl.when(jnp.logical_not(has[sx]))
        def _():
            for c in range(2):
                (x0, x1)[c][m] = jnp.zeros((rows + 2 * PAD, cols), jnp.float32)
            eb[m] = zero
            qb[m] = zero

    def copy(src_ref, dst_ref, device, slot, t):
        return pltpu.make_async_remote_copy(
            src_ref=src_ref, dst_ref=dst_ref, send_sem=send.at[slot, t], recv_sem=recv.at[slot, t],
            device_id=device, device_id_type=MESH,
        )


    def msg_x(sx, t):
        return copy(x1.at[edge_m[sx] + 1, pl.ds(PAD, rows)], xg.at[1 - sx, t], {"gx": x_to[sx]}, X + sx, t)

    def msg_y(sy, t):
        return copy(jb.at[sy, t], jr.at[1 - sy, t], {"gy": y_to[sy]}, Y + sy, t)

    def msg_z(zd, t):
        return copy(pk.at[t], zr.at[zd, t], {"gz": z_to[zd]}, Z + zd, t)

    def msg_xy(sx, sy, t):
        return copy(
            jb.at[sy, t, edge_m[sx]], xyr.at[1 - sx, 1 - sy, t], {"gx": x_to[sx], "gy": y_to[sy]}, XY + 2 * sx + sy, t
        )

    def msg_yz(sy, zd, t):
        return copy(yzs.at[sy, t], yzr.at[1 - sy, zd, t], {"gy": y_to[sy], "gz": z_to[zd]}, YZ + 2 * sy + zd, t)

    def msg_xz(sx, zd, t):
        return copy(
            pk.at[t, edge_m[sx]], xzr.at[1 - sx, zd, t], {"gx": x_to[sx], "gz": z_to[zd]}, XZ + 2 * sx + zd, t
        )

    def msg_sx(sx):
        return copy(
            s0.at[edge_m[sx] + 1, pl.ds(PAD, rows)], s0.at[(nm + 1, 0)[sx], pl.ds(PAD, rows)],
            {"gx": x_to[sx]}, SX + sx, 0,
        )

    def msg_sy(sy):
        return copy(sys_.at[sy], syr.at[1 - sy], {"gy": y_to[sy]}, SY + sy, 0)

    def msg_sz(zd):
        return copy(sqs, szr.at[zd], {"gz": z_to[zd]}, SZ + zd, 0)

    def send_far(t):
        for sy in range(2):
            for zd in range(nz):
                msg_yz(sy, zd, t).start()
        for sx in range(2):

            @pl.when(has[sx])
            def _():
                for sy in range(2):
                    msg_xy(sx, sy, t).start()

        for sy in range(2):
            msg_y(sy, t).start()

    def send_x(t):
        for sx in range(2):

            @pl.when(has[sx])
            def _():
                msg_x(sx, t).start()

    def send_z(t):
        for sx in range(2):

            @pl.when(has[sx])
            def _():
                for zd in range(nz):
                    msg_xz(sx, zd, t).start()

        for zd in range(nz):
            msg_z(zd, t).start()

    def rows_of(g, shift=0):
        return pl.ds(PAD + 8 * g + shift, 8)

    def keep_rows(t, m, g, y, sy):
        if sy == 0:
            jb[0, t, m] = y[0:2]
            yzs[0, t, pl.ds(m, 1), :] = roll(y, 4 * hi_quad + 2)[0:1]
        else:
            jb[1, t, m] = y[6:8]
            yzs[1, t, pl.ds(m, 1), :] = roll(y, -2)[7:8]

    def packed(acc, g, y):
        return jnp.where(quad == g, roll(y, 4 * g + 2), acc)

    def field_rows(m, groups):
        for g in groups:
            rs = pl.ds(8 * g, 8)
            x1[m + 1, rows_of(g), :] = jnp.where(odd, fv[2 * m, rs, :], fv[2 * m + 1, rs, :])

    def field_plane(m, carry):
        load_field(m).wait()
        field_rows(m, inner)
        return carry

    def several(lo, hi, n, body):
        n = max(k for k in range(1, n + 1) if (hi - lo) % k == 0)

        def step(i, carry):
            for k in range(n):
                body(lo + n * i + k)
            return carry

        lax.fori_loop(0, (hi - lo) // n, step, 0)

    def pack_plane(t, m):
        acc = [zero] * 4
        for g in range(ng):
            acc[g % 4] = packed(acc[g % 4], g, x1[m + 1, rows_of(g), :])
        pk[t, m] = (acc[0] + acc[1]) + (acc[2] + acc[3])

    def pack(t):
        several(0, nm, 4, functools.partial(pack_plane, t))

    inner = range(1, ng - 1)

    def source_plane(m, carry):
        load(s_hbm, sv, ssem, m).wait()
        acc = [zero] * 4
        for g in range(ng):
            rs = pl.ds(8 * g, 8)
            low, high = sv[2 * m, rs, :], sv[2 * m + 1, rs, :]
            red = jnp.where(odd, high, low)
            s0[m + 1, rows_of(g), :] = red
            s1[m, rows_of(g), :] = jnp.where(odd, low, high)
            acc[g % 4] = packed(acc[g % 4], g, red)
            if g == 0:
                sys_[0, pl.ds(m, 1), :] = red[0:1]
            if g == ng - 1:
                sys_[1, pl.ds(m, 1), :] = red[7:8]
        sqs[m] = (acc[0] + acc[1]) + (acc[2] + acc[3])
        return carry

    with jax.named_scope("ends"):
        for sy, g in ((0, 0), (1, ng - 1)):
            load_ends(sy).wait()
            for m in range(nm):
                field_rows(m, (g,))
                keep_rows(0, m, g, x1[m + 1, rows_of(g), :], sy)
    near = [h.astype(jnp.int32) for h in has]
    with jax.named_scope("barrier"):
        pl.semaphore_wait(barrier, 2 + 3 * nz + (near[0] + near[1]) * (3 + nz))
    send_far(0)
    with jax.named_scope("field"):
        for m in edge_m:
            field_plane(m, 0)
        send_x(0)
        lax.fori_loop(1, nm - 1, field_plane, 0)
    with jax.named_scope("pack"):
        pack(0)
    send_z(0)
    with jax.named_scope("source"):
        lax.fori_loop(0, nm, source_plane, 0)
    for sy in range(2):
        msg_sy(sy).start()
    for zd in range(nz):
        msg_sz(zd).start()
    for sx in range(2):

        @pl.when(has[sx])
        def _():
            msg_sx(sx).start()

    def tile(c, m, g, edge, side=None):
        v = (x1, x0)[c]
        rs = rows_of(g)
        here = v[m + 1, rs, :]
        if side is None:
            below, above = v[m, rs, :], v[m + 2, rs, :]
            beside = jnp.where(odd, above, below) if c == 0 else jnp.where(odd, below, above)
        else:
            beside = v[m + 1 + side, rs, :]
        given = s0[m + 1, rs, :] if c == 0 else s1[m, rs, :]
        total = (given + here) + (beside + v[m + 1, rows_of(g, -1), :])
        total = total + v[m + 1, rows_of(g, 1), :]
        total = total + jnp.where(first, edge, roll(here, 1))
        total = total + jnp.where(final_lane, edge, roll(here, -1))
        return total * jnp.float32(SIXTH)

    def edge_at(v, g):
        return roll(v, -(4 * g + 2))

    def red_plane(m, groups, side=None):
        v = eb[m + 1]
        for g in groups:
            x0[m + 1, rows_of(g), :] = tile(0, m, g, edge_at(v, g), side)

    def put(m, g, y, final):
        if final:
            red = x0[m + 1, rows_of(g), :]
            rs = pl.ds(8 * g, 8)
            ov[2 * m, rs, :] = jnp.where(odd, y, red)
            ov[2 * m + 1, rs, :] = jnp.where(odd, red, y)
        else:
            x1[m + 1, rows_of(g), :] = y

    def black_plane(m, groups, final):
        v = er[m]
        for g in groups:
            put(m, g, tile(1, m, g, edge_at(v, g)), final)

    def swapped(lo, hi):
        return jnp.where(pos1, roll(hi, -1), roll(lo, 1))

    for t in range(SWEEPS):
        final = t == SWEEPS - 1
        hi_z = nz - 1
        with jax.named_scope("waitz"):
            for zd in range(nz):
                msg_z(zd, t).wait_recv()
        for m in range(nm):
            lo, hi = zr[0, t, m], zr[hi_z, t, m]
            qb[m + 1] = jnp.where(low_half, lo, hi)
            eb[m + 1] = swapped(lo, hi)
        with jax.named_scope("P1"):
            several(1, nm - 1, 3, lambda m: red_plane(m, inner))

        with jax.named_scope("P2x"):
            for sx in range(2):
                m, at = ((-1, 0), (nm, nm + 1))[sx]

                @pl.when(has[sx])
                def _():
                    for zd in range(nz):
                        msg_xz(1 - sx, zd, t).wait_recv()
                    lo, hi = xzr[sx, 0, t], xzr[sx, hi_z, t]
                    qb[at] = jnp.where(low_half, lo, hi)
                    eb[at] = swapped(lo, hi)
                    msg_x(1 - sx, t).wait_recv()
                    if t == 0:
                        msg_sx(1 - sx).wait_recv()
                    x1[at, pl.ds(PAD, rows), :] = xg[sx, t]
                    red_plane(m, inner, (1, -1)[sx])

        with jax.named_scope("P2e"):
            for m in edge_m:
                red_plane(m, inner)

        with jax.named_scope("P3wait"):
            if t == 0:
                for zd in range(nz):
                    msg_sz(zd).wait_recv()
                for m in range(nm):
                    sq[m] = jnp.where(low_half, szr[0, m], szr[hi_z, m])
                for sy in range(2):
                    msg_sy(sy).wait_recv()
                    for m in range(nm):
                        s0[m + 1, pl.ds((PAD + rows, PAD - 1)[sy], 1), :] = syr[1 - sy, pl.ds(m, 1), :]
            for sy in range(2):
                msg_y(sy, t).wait_recv()
                for m in range(nm):
                    x1[m + 1, pl.ds((PAD + rows, PAD - 2)[sy], 2), :] = jr[1 - sy, t, m]
            for sx in range(2):

                @pl.when(has[sx])
                def _():
                    for sy in range(2):
                        msg_xy(1 - sx, sy, t).wait_recv()
                        x1[(0, nm + 1)[sx], pl.ds((PAD + rows, PAD - 2)[sy], 2), :] = xyr[sx, 1 - sy, t]

            low8 = lax.rem(lax.broadcasted_iota(jnp.int32, (nm, cols), 1), 4)
            for sy in range(2):
                for zd in range(nz):
                    msg_yz(sy, zd, t).wait_recv()
                lo, hi = yzr[1 - sy, 0, t], yzr[1 - sy, hi_z, t]
                yzb[1 - sy] = jnp.where(low8 < 2, lo, hi)
                yzb[2 + 1 - sy] = jnp.where(low8 == 1, pltpu.roll(hi, last, 1), pltpu.roll(lo, 1, 1))

        def spread(k, m):
            return jnp.broadcast_to(yzb[k, pl.ds(m, 1), :], (8, cols))

        with jax.named_scope("P3red"):
            for sx in range(2):
                m = (-1, nm)[sx]

                @pl.when(has[sx])
                def _():
                    red_plane(m, (0, ng - 1), (1, -1)[sx])

            for m in range(nm):
                red_plane(m, (0, ng - 1))
                for g, k in ((-1, 2), (ng, 3)):
                    x0[m + 1, rows_of(g), :] = tile(0, m, g, edge_at(spread(k, m), g))
                own, q = pk[t, m], qb[m + 1]
                zsum = roll(jnp.where(pos0, q, own), 1) + roll(jnp.where(pos3, q, own), -1)
                beside = jnp.where(odd_q, qb[m + 2], qb[m])
                up = jnp.where(bottom, roll(jnp.where(in_lo, spread(0, m), q), 4), q)
                down = jnp.where(top, roll(jnp.where(in_hi, spread(1, m), q), -4), q)
                total = (sq[m] + q) + (beside + pltpu.roll(up, 1, 0)) + (pltpu.roll(down, 7, 0) + zsum)
                red = total * jnp.float32(SIXTH)
                er[m] = swapped(red, red)

        if not final:
            for sx in range(2):

                @pl.when(has[sx])
                def _():
                    msg_x(sx, t).wait_send()

        with jax.named_scope("P3blk"):
            for m in range(nm):
                v = er[m]
                for sy, g in ((0, 0), (1, ng - 1)):
                    y = tile(1, m, g, edge_at(v, g))
                    put(m, g, y, final)
                    if not final:
                        keep_rows(t + 1, m, g, y, sy)

        if not final:
            send_far(t + 1)
        with jax.named_scope("P4"):
            for m in edge_m:
                black_plane(m, inner, final)
        if not final:
            send_x(t + 1)

        with jax.named_scope("P5"):
            several(1, nm - 1, 3, lambda m: black_plane(m, inner, final))
        if not final:
            with jax.named_scope("pack"):
                pack(t + 1)
            send_z(t + 1)

    for sy in range(2):
        msg_sy(sy).wait_send()
    for zd in range(nz):
        msg_sz(zd).wait_send()
    for t in range(SWEEPS):
        for sy in range(2):
            msg_y(sy, t).wait_send()
            for zd in range(nz):
                msg_yz(sy, zd, t).wait_send()
        for zd in range(nz):
            msg_z(zd, t).wait_send()
    for sx in range(2):

        @pl.when(has[sx])
        def _():
            msg_sx(sx).wait_send()
            msg_x(sx, SWEEPS - 1).wait_send()
            for t in range(SWEEPS):
                for sy in range(2):
                    msg_xy(sx, sy, t).wait_send()
                for zd in range(nz):
                    msg_xz(sx, zd, t).wait_send()


def solution(mesh):
    sizes = tuple(mesh.shape[a] for a in ("gx", "gy", "gz"))

    def on_device(field, source):
        planes, rows, cols = field.shape
        nm, ng, nz = planes // 2, rows // 8, 1 if sizes[2] == 2 else 2
        assert planes % 4 == 0 and nm >= 4 and rows % 8 == 0 and cols == 128 and 4 * ng <= cols
        f32 = jnp.float32
        vm = lambda *shape: pltpu.VMEM(shape, f32)
        return pl.pallas_call(
            functools.partial(kernel, sizes),
            out_shape=jax.ShapeDtypeStruct(field.shape, f32),
            in_specs=[pl.BlockSpec(memory_space=pltpu.HBM)] * 2,
            out_specs=pl.BlockSpec(memory_space=pltpu.VMEM),
            scratch_shapes=[
                vm(*field.shape),
                vm(*field.shape),
                vm(nm + 2, rows + 2 * PAD, cols),
                vm(nm + 2, rows + 2 * PAD, cols),
                vm(nm + 2, rows + 2 * PAD, cols),
                vm(nm, rows + 2 * PAD, cols),
                vm(nm + 2, 8, cols),
                vm(nm, 8, cols),
                vm(nm + 2, 8, cols),
                vm(nm, 8, cols),
                vm(4, nm, cols),
                vm(nm, 8, cols),
                vm(SWEEPS, nm, 8, cols),
                vm(2, SWEEPS, nm, 2, cols),
                vm(2, SWEEPS, nm, cols),
                vm(2, nm, cols),
                vm(2, SWEEPS, rows, cols),
                vm(2, SWEEPS, nm, 2, cols),
                vm(nz, SWEEPS, nm, 8, cols),
                vm(2, 2, SWEEPS, 2, cols),
                vm(2, nz, SWEEPS, nm, cols),
                vm(2, nz, SWEEPS, 8, cols),
                vm(2, nm, cols),
                vm(nz, nm, 8, cols),
                pltpu.SemaphoreType.DMA((24, SWEEPS)),
                pltpu.SemaphoreType.DMA((24, SWEEPS)),
                pltpu.SemaphoreType.DMA((nm + 2,)),
                pltpu.SemaphoreType.DMA((nm,)),
            ],
            compiler_params=pltpu.CompilerParams(
                collective_id=0, has_side_effects=True, vmem_limit_bytes=50 * 1024 * 1024
            ),
        )(field, source)

    spec = P("gx", "gy", "gz")
    return jax.shard_map(on_device, mesh=mesh, in_specs=(spec, spec), out_specs=spec, check_vma=False)
```

time: 30.4 us -> 28.5 us (0.938)
  Pallas kernels: 28.9 us -> 27 us
    pallas_call x1, Pallas kernels: 28.9 us -> 27 us  [on_device(): pl.pallas_call(functools.partial(kernel, sizes), out_shape=jax.ShapeDtype...]
where the time goes in v2:
time: 28.5 us; the launch traced here: 28.3 us
  Pallas kernels  27 us (95%)
  local copies, waits for them, and re-layouts  1.32 us (5%)
    pallas_call x1, Pallas kernels, on_device(): pl.pallas_call(functools.partial(kernel, sizes), out_shape=jax.ShapeDtype...  27 us
    unnamed x1, local copies, waits for them, and re-layouts  1.32 us

profile of v2, /device:TPU:1, one launch (start us, length us, event | category | flops | bytes accessed | tf_op | source)
XLA Modules:
  0.0 28.3 jit_solution(17936053871546388594)
XLA Ops:
  0.0 27.0 %shard_map.28 = f32[16,256,128]{2,1,0:T(8,128)S(1)} custom-call(f32[16,256,128]{2,1,0:T(8,128)} %f_hbm.1, f32[16,256,128]{2,1,0:T(8,128)} %s_hbm.1), custom_call_target="tpu_custom_call" | custom-call | tf_op jit(solution)/shard_map/pallas_call | solution.py:459
  27.0 1.3 %copy.4 = f32[16,256,128]{2,1,0:T(8,128)} copy(f32[16,256,128]{2,1,0:T(8,128)S(1)} %shard_map.28) | data formatting | bytes 4194304

commit v3 on v2

v3 whole, which is shorter than its diff:
```python
import functools

import jax
import jax.numpy as jnp
from jax import lax
from jax.experimental import pallas as pl
from jax.experimental.pallas import tpu as pltpu
from jax.sharding import PartitionSpec as P

SWEEPS = 3
MESH = pl.DeviceIdType.MESH
PAD = 16


def slots(nz):
    sizes = dict(X=4, Y=2, Z=4 * nz, XY=4, YZ=2 * nz, XZ=2 * nz, SX=2, SY=2, SZ=nz)
    first, total = {}, 0
    for name, size in sizes.items():
        if name == "SX":
            rounds = total
        first[name], total = total, total + size
    return first, rounds, total

SIXTH = 1.0 / 6.0


def kernel(
    sizes, f_hbm, s_hbm, ov, fv, sv, x0, x1, s0, s1, eb, er, rq, qb, sq, yzb, sqs,
    pk, jb, yzs, sys_, sxs, sxr, xg, jr, zr, xyr, yzr, xzr, syr, szr, send, recv, fsem, ssem,
):
    ngx, ngy, ngz = sizes
    planes, rows, cols = f_hbm.shape
    nm = planes // 2
    ng = rows // 8
    gx, gy, gz = (lax.axis_index(a) for a in ("gx", "gy", "gz"))
    has = (gx > 0, gx < ngx - 1)
    nz = 1 if ngz == 2 else 2
    y_to = (lax.rem(gy + ngy - 1, ngy), lax.rem(gy + 1, ngy))
    z_to = (lax.rem(gz + 1, ngz), lax.rem(gz + ngz - 1, ngz))[:nz]
    x_to = (gx - 1, gx + 1)
    last = cols - 1
    edge_m = (0, nm - 1)
    mid = nm // 2
    parts = ((0, 1), (nm - 1, nm), (1, mid), (mid, nm - 1))
    middle = parts[2:]

    def load_source(part):
        lo, hi = parts[part]
        at = pl.ds(2 * lo, 2 * (hi - lo))
        return pltpu.make_async_copy(s_hbm.at[at], sv.at[at], ssem.at[part])

    def load_ends(sy):
        rs = pl.ds((0, rows - 8)[sy], 8)
        return pltpu.make_async_copy(f_hbm.at[:, rs], fv.at[:, rs], fsem.at[4 + sy])

    def load_field(part):
        lo, hi = parts[part]
        at = (pl.ds(2 * lo, 2 * (hi - lo)), pl.ds(8, rows - 16))
        return pltpu.make_async_copy(f_hbm.at[at], fv.at[at], fsem.at[part])

    for sy in range(2):
        load_ends(sy).start()
    for part in range(4):
        load_field(part).start()
    for part in range(4):
        load_source(part).start()

    barrier = pltpu.get_barrier_semaphore()

    def greet(device):
        pl.semaphore_signal(barrier, inc=1, device_id=device, device_id_type=MESH)

    for y in y_to:
        greet({"gy": y})
        for z in z_to:
            greet({"gy": y, "gz": z})
    for z in z_to:
        greet({"gz": z})
    for sx in range(2):

        @pl.when(has[sx])
        def _():
            greet({"gx": x_to[sx]})
            for y in y_to:
                greet({"gx": x_to[sx], "gy": y})
            for z in z_to:
                greet({"gx": x_to[sx], "gz": z})

    sub = lax.broadcasted_iota(jnp.int32, (8, cols), 0)
    lane = lax.broadcasted_iota(jnp.int32, (8, cols), 1)
    odd = lax.rem(sub + lane, 2) == 1
    first, final_lane = lane == 0, lane == last
    quad = lax.div(lane, 4)
    pos = lax.rem(lane, 4)
    pos0, pos1, pos3, low_half = pos == 0, pos == 1, pos == 3, pos < 2
    odd_q = lax.rem(sub + jnp.where(pos1, 1, 0), 2) == 1
    top, bottom = sub == 0, sub == 7
    no_up = top & (quad == 0)
    no_down = bottom & (quad == ng - 1)
    ends = first | final_lane
    odd_lane = lax.rem(lax.broadcasted_iota(jnp.int32, (rows // 2, cols), 1), 2) == 1
    zero = jnp.zeros((8, cols), jnp.float32)

    def roll(v, by):
        by = by % cols
        return v if by == 0 else pltpu.roll(v, by, 1)

    for sx in range(2):
        m = (0, nm + 1)[sx]

        @pl.when(jnp.logical_not(has[sx]))
        def _():
            for c in range(2):
                (x0, x1)[c][m] = jnp.zeros((rows + 2 * PAD, cols), jnp.float32)
            eb[m] = zero
            qb[m] = zero

    base, rounds, total_slots = slots(nz)

    def copy(src_ref, dst_ref, device, kind, k, t):
        slot = base[kind] + k
        return pltpu.make_async_remote_copy(
            src_ref=src_ref, dst_ref=dst_ref, send_sem=send.at[slot], recv_sem=recv.at[slot + (t % 2) * total_slots],
            device_id=device, device_id_type=MESH,
        )


    def msg_x(sx, half, t):
        start = half * (rows // 2)
        return copy(
            x1.at[edge_m[sx] + 1, pl.ds(PAD + start, rows // 2)], xg.at[1 - sx, t, pl.ds(start, rows // 2)],
            {"gx": x_to[sx]}, "X", 2 * sx + half, t,
        )

    def msg_y(sy, t):
        return copy(jb.at[sy, t], jr.at[1 - sy, t], {"gy": y_to[sy]}, "Y", sy, t)

    def msg_z(zd, part, t):
        lo, hi = parts[part]
        at = pl.ds(lo, hi - lo)
        return copy(pk.at[t, at], zr.at[zd, t, at], {"gz": z_to[zd]}, "Z", 4 * zd + part, t)

    def msg_xy(sx, sy, t):
        return copy(
            jb.at[sy, t, edge_m[sx]], xyr.at[1 - sx, 1 - sy, t], {"gx": x_to[sx], "gy": y_to[sy]}, "XY", 2 * sx + sy, t
        )

    def msg_yz(sy, zd, t):
        return copy(yzs.at[sy, t], yzr.at[1 - sy, zd, t], {"gy": y_to[sy], "gz": z_to[zd]}, "YZ", nz * sy + zd, t)

    def msg_xz(sx, zd, t):
        return copy(
            pk.at[t, edge_m[sx]], xzr.at[1 - sx, zd, t], {"gx": x_to[sx], "gz": z_to[zd]}, "XZ", nz * sx + zd, t
        )

    def msg_sx(sx):
        return copy(sxs.at[sx], sxr.at[1 - sx], {"gx": x_to[sx]}, "SX", sx, 0)

    def source_face(sx):
        even = s0[edge_m[sx] + 1, pl.ds(PAD, rows // 2, stride=2), :]
        uneven = s0[edge_m[sx] + 1, pl.ds(PAD + 1, rows // 2, stride=2), :]
        sxs[sx] = jnp.where(odd_lane, uneven, even) if sx == 0 else jnp.where(odd_lane, even, uneven)

    def msg_sy(sy):
        return copy(sys_.at[sy], syr.at[1 - sy], {"gy": y_to[sy]}, "SY", sy, 0)

    def msg_sz(zd):
        return copy(sqs, szr.at[zd], {"gz": z_to[zd]}, "SZ", zd, 0)

    def send_far(t):
        for sy in range(2):
            for zd in range(nz):
                msg_yz(sy, zd, t).start()
        for sx in range(2):

            @pl.when(has[sx])
            def _():
                for sy in range(2):
                    msg_xy(sx, sy, t).start()

        for sy in range(2):
            msg_y(sy, t).start()

    def send_x(half, t):
        for sx in range(2):

            @pl.when(has[sx])
            def _():
                msg_x(sx, half, t).start()

    def send_z(part, t):
        for zd in range(nz):
            msg_z(zd, part, t).start()

    def send_edges(t):
        for sx in range(2):

            @pl.when(has[sx])
            def _():
                for zd in range(nz):
                    msg_xz(sx, zd, t).start()

        for part in range(2):
            send_z(part, t)

    def sent(t):
        for sy in range(2):
            msg_y(sy, t).wait_send()
            if t == 0:
                msg_sy(sy).wait_send()
            for zd in range(nz):
                msg_yz(sy, zd, t).wait_send()
        for zd in range(nz):
            if t == 0:
                msg_sz(zd).wait_send()
            for part in range(4):
                msg_z(zd, part, t).wait_send()
        for sx in range(2):

            @pl.when(has[sx])
            def _():
                if t == 0:
                    msg_sx(sx).wait_send()
                for half in range(2):
                    msg_x(sx, half, t).wait_send()
                for sy in range(2):
                    msg_xy(sx, sy, t).wait_send()
                for zd in range(nz):
                    msg_xz(sx, zd, t).wait_send()

    def rows_of(g, shift=0):
        return pl.ds(PAD + 8 * g + shift, 8)

    def keep_rows(t, m, y, sy):
        jb[sy, t, m] = y[0:2] if sy == 0 else y[6:8]
        yzs[sy, t, pl.ds(m, 1), :] = y[0:1] if sy == 0 else y[7:8]

    def packed(acc, g, y):
        return jnp.where(quad == g, roll(y, 4 * g + 2), acc)

    def field_rows(m, groups):
        for g in groups:
            rs = pl.ds(8 * g, 8)
            x1[m + 1, rows_of(g), :] = jnp.where(odd, fv[2 * m, rs, :], fv[2 * m + 1, rs, :])

    def field_plane(m):
        field_rows(m, inner)

    def several(lo, hi, n, body):
        n = max(k for k in range(1, n + 1) if (hi - lo) % k == 0)

        def step(i, carry):
            for k in range(n):
                body(lo + n * i + k)
            return carry

        lax.fori_loop(0, (hi - lo) // n, step, 0)

    def pack_plane(t, m):
        acc = [zero] * 4
        for g in range(ng):
            acc[g % 4] = packed(acc[g % 4], g, x1[m + 1, rows_of(g), :])
        pk[t, m] = (acc[0] + acc[1]) + (acc[2] + acc[3])

    def pack(part, t):
        with jax.named_scope("pack"):
            several(*middle[part], 4, functools.partial(pack_plane, t))
        send_z(2 + part, t)

    def pack_edges(t):
        with jax.named_scope("packe"):
            for m in edge_m:
                pack_plane(t, m)
        send_edges(t)

    inner = range(1, ng - 1)

    def source_plane(m):
        acc = [zero] * 4
        for g in range(ng):
            rs = pl.ds(8 * g, 8)
            low, high = sv[2 * m, rs, :], sv[2 * m + 1, rs, :]
            red = jnp.where(odd, high, low)
            s0[m + 1, rows_of(g), :] = red
            s1[m, rows_of(g), :] = jnp.where(odd, low, high)
            acc[g % 4] = packed(acc[g % 4], g, red)
            if g == 0:
                sys_[0, pl.ds(m, 1), :] = red[0:1]
            if g == ng - 1:
                sys_[1, pl.ds(m, 1), :] = red[7:8]
        sqs[m] = (acc[0] + acc[1]) + (acc[2] + acc[3])

    with jax.named_scope("ends"):
        for sy, g in ((0, 0), (1, ng - 1)):
            load_ends(sy).wait()
            for m in range(nm):
                field_rows(m, (g,))
                keep_rows(0, m, x1[m + 1, rows_of(g), :], sy)
    near = [h.astype(jnp.int32) for h in has]
    with jax.named_scope("barrier"):
        pl.semaphore_wait(barrier, 2 + 3 * nz + (near[0] + near[1]) * (3 + nz))
    send_far(0)
    with jax.named_scope("field"):
        for part in range(2):
            load_field(part).wait()
            field_plane(edge_m[part])
        for half in range(2):
            send_x(half, 0)
    pack_edges(0)
    for part in range(2):
        with jax.named_scope("field"):
            load_field(2 + part).wait()
            several(*middle[part], 3, field_plane)
        pack(part, 0)
    with jax.named_scope("source"):
        for part in range(4):
            load_source(part).wait()
        several(0, nm, 4, source_plane)
    for sx in range(2):

        @pl.when(has[sx])
        def _():
            source_face(sx)
            msg_sx(sx).start()

    for sy in range(2):
        msg_sy(sy).start()
    for zd in range(nz):
        msg_sz(zd).start()

    def tile(c, m, g, edge, side=None, right=None):
        v = (x1, x0)[c]
        rs = rows_of(g)
        here = v[m + 1, rs, :]
        if side is None:
            below, above = v[m, rs, :], v[m + 2, rs, :]
            beside = jnp.where(odd, above, below) if c == 0 else jnp.where(odd, below, above)
        else:
            beside = v[m + 1 + side, rs, :]
        given = s0[m + 1, rs, :] if c == 0 else s1[m, rs, :]
        total = (given + here) + (beside + v[m + 1, rows_of(g, -1), :])
        total = total + v[m + 1, rows_of(g, 1), :]
        total = total + jnp.where(first, edge, roll(here, 1))
        total = total + jnp.where(final_lane, edge if right is None else right, roll(here, -1))
        return total * jnp.float32(SIXTH)

    def edge_at(v, g):
        return roll(v, -(4 * g + 2))

    def red_plane(m, groups, side=None):
        v = eb[m + 1]
        for g in groups:
            x0[m + 1, rows_of(g), :] = tile(0, m, g, edge_at(v, g), side)

    def put(m, g, y, final):
        if final:
            red = x0[m + 1, rows_of(g), :]
            rs = pl.ds(8 * g, 8)
            ov[2 * m, rs, :] = jnp.where(odd, y, red)
            ov[2 * m + 1, rs, :] = jnp.where(odd, red, y)
        else:
            x1[m + 1, rows_of(g), :] = y

    def black_plane(m, groups, final):
        v = er[m]
        for g in groups:
            put(m, g, tile(1, m, g, edge_at(v, g)), final)

    def swapped(lo, hi):
        return jnp.where(pos1, roll(hi, -1), roll(lo, 1))

    lane8 = lax.broadcasted_iota(jnp.int32, (nm, cols), 1)
    hi_z = nz - 1

    def ghost_plane(sx, groups):
        m = (-1, nm)[sx]
        v = eb[m + 1]
        for g in groups:
            y = tile(0, m, g, edge_at(v, g), (1, -1)[sx])
            x0[m + 1, rows_of(g), :] = jnp.where(has[sx], y, 0.0)

    def take_z(part, t):
        with jax.named_scope("waitz"):
            for zd in range(nz):
                msg_z(zd, part, t).wait_recv()
        for m in range(*parts[part]):
            lo, hi = zr[0, t, m], zr[hi_z, t, m]
            qb[m + 1] = jnp.where(low_half, lo, hi)
            eb[m + 1] = swapped(lo, hi)

    z_early = lax.rem(gx, 2) == 1

    def close_inner(t):
        for part in range(2):
            take_z(2 + part, t)
            with jax.named_scope("P1z"):
                several(*middle[part], 3, close_plane)

    def pre_red(t):
        if t == 0:
            for zd in range(nz):
                msg_sz(zd).wait_recv()
            for m in range(nm):
                sq[m] = jnp.where(low_half, szr[0, m], szr[hi_z, m])
        for m in range(nm):
            own, q = pk[t, m], qb[m + 1]
            zsum = roll(jnp.where(pos0, q, own), 1) + roll(jnp.where(pos3, q, own), -1)
            beside = jnp.where(odd_q, qb[m + 2], qb[m])
            up = jnp.where(bottom, roll(q, 4), q)
            up = jnp.where(no_up, 0.0, pltpu.roll(up, 1, 0))
            down = jnp.where(top, roll(q, -4), q)
            down = jnp.where(no_down, 0.0, pltpu.roll(down, 7, 0))
            rq[m] = (sq[m] + q) + (beside + up) + (down + zsum)

    def open_plane(m):
        for g in inner:
            x0[m + 1, rows_of(g), :] = tile(0, m, g, 0.0)

    def close_plane(m):
        v = eb[m + 1] * jnp.float32(SIXTH)
        for g in inner:
            rs = rows_of(g)
            x0[m + 1, rs, :] = x0[m + 1, rs, :] + jnp.where(ends, edge_at(v, g), 0.0)

    for t in range(SWEEPS):
        final = t == SWEEPS - 1
        with jax.named_scope("P1"):
            several(1, nm - 1, 3, open_plane)
        with jax.named_scope("sent"):
            sent(t)
        for part in range(2):
            take_z(part, t)

        @pl.when(z_early)
        def _():
            close_inner(t)

        for half in range(2):
            start = half * (rows // 2)
            groups = (inner[: ng // 2 - 2], inner[ng // 2 - 2 :])[half]
            with jax.named_scope("waitx"):
                for sx in range(2):
                    at = (0, nm + 1)[sx]

                    @pl.when(has[sx])
                    def _():
                        if half == 0:
                            for zd in range(nz):
                                msg_xz(1 - sx, zd, t).wait_recv()
                            lo, hi = xzr[sx, 0, t], xzr[sx, hi_z, t]
                            qb[at] = jnp.where(low_half, lo, hi)
                            eb[at] = swapped(lo, hi)
                            if t == 0:
                                msg_sx(1 - sx).wait_recv()
                                for row in range(2):
                                    s0[at, pl.ds(PAD + row, rows // 2, stride=2), :] = sxr[sx]
                        msg_x(1 - sx, half, t).wait_recv()
                        x1[at, pl.ds(PAD + start, rows // 2), :] = xg[sx, t, pl.ds(start, rows // 2), :]

            with jax.named_scope("P2"):
                for sx in range(2):
                    ghost_plane(sx, groups)
                    red_plane(edge_m[sx], groups)

        @pl.when(jnp.logical_not(z_early))
        def _():
            close_inner(t)

        with jax.named_scope("prered"):
            pre_red(t)

        with jax.named_scope("waity"):
            for sy in range(2):
                if t == 0:
                    msg_sy(sy).wait_recv()
                    for m in range(nm):
                        s0[m + 1, pl.ds((PAD + rows, PAD - 1)[sy], 1), :] = syr[1 - sy, pl.ds(m, 1), :]
                msg_y(sy, t).wait_recv()
                for m in range(nm):
                    x1[m + 1, pl.ds((PAD + rows, PAD - 2)[sy], 2), :] = jr[1 - sy, t, m]
        with jax.named_scope("P3a"):
            for m in range(nm):
                red_plane(m, (0, ng - 1))
        with jax.named_scope("waitfar"):
            for sx in range(2):

                @pl.when(has[sx])
                def _():
                    for sy in range(2):
                        msg_xy(1 - sx, sy, t).wait_recv()
                        x1[(0, nm + 1)[sx], pl.ds((PAD + rows, PAD - 2)[sy], 2), :] = xyr[sx, 1 - sy, t]

            for sy in range(2):
                for zd in range(nz):
                    msg_yz(sy, zd, t).wait_recv()

        with jax.named_scope("P3b"):
            for side in range(2):
                lo, hi = yzr[side, 0, t], yzr[side, hi_z, t]
                yzb[side] = pltpu.roll(jnp.where(lane8 >= cols // 2, lo, hi), (2, (4 * ng - 2) % cols)[side], 1)
                yzb[2 + side] = jnp.where(lane8 == 0, pltpu.roll(lo, 1, 1), pltpu.roll(hi, last, 1))
            for sx in range(2):
                ghost_plane(sx, (0, ng - 1))
            for m in range(nm):
                for g, k in ((-1, 2), (ng, 3)):
                    x0[m + 1, rows_of(g), :] = tile(0, m, g, jnp.broadcast_to(yzb[k, pl.ds(m, 1), :], (8, cols)))
            for m in range(nm):
                total = rq[m] + jnp.where(no_up, jnp.broadcast_to(yzb[0, pl.ds(m, 1), :], (8, cols)), 0.0)
                total = total + jnp.where(no_down, jnp.broadcast_to(yzb[1, pl.ds(m, 1), :], (8, cols)), 0.0)
                rq[m] = total * jnp.float32(SIXTH)
            for m in range(nm):
                red = rq[m]
                for sy, g in ((0, 0), (1, ng - 1)):
                    y = tile(1, m, g, roll(red, -(4 * g + 1)), None, roll(red, -(4 * g + 3)))
                    put(m, g, y, final)
                    if not final:
                        keep_rows(t + 1, m, y, sy)

        if not final:
            send_far(t + 1)
        with jax.named_scope("P4"):
            for m in range(nm):
                er[m] = swapped(rq[m], rq[m])
            for half, groups in enumerate((inner[: ng // 2 - 1], inner[ng // 2 - 1 :])):
                for m in edge_m:
                    black_plane(m, groups, final)
                if not final:
                    send_x(half, t + 1)
        if not final:
            pack_edges(t + 1)
        for part in range(2):
            with jax.named_scope("P5"):
                several(*middle[part], 3, lambda m: black_plane(m, inner, final))
            if not final:
                pack(part, t + 1)


def solution(mesh):
    sizes = tuple(mesh.shape[a] for a in ("gx", "gy", "gz"))

    def on_device(field, source):
        planes, rows, cols = field.shape
        nm, ng, nz = planes // 2, rows // 8, 1 if sizes[2] == 2 else 2
        assert planes % 4 == 0 and nm >= 4 and rows % 8 == 0 and cols == 128 and 4 * ng <= cols
        _, rounds, total_slots = slots(nz)
        f32 = jnp.float32
        vm = lambda *shape: pltpu.VMEM(shape, f32)
        return pl.pallas_call(
            functools.partial(kernel, sizes),
            out_shape=jax.ShapeDtypeStruct(field.shape, f32),
            in_specs=[pl.BlockSpec(memory_space=pltpu.HBM)] * 2,
            out_specs=pl.BlockSpec(memory_space=pltpu.VMEM),
            scratch_shapes=[
                vm(*field.shape),
                vm(*field.shape),
                vm(nm + 2, rows + 2 * PAD, cols),
                vm(nm + 2, rows + 2 * PAD, cols),
                vm(nm + 2, rows + 2 * PAD, cols),
                vm(nm, rows + 2 * PAD, cols),
                vm(nm + 2, 8, cols),
                vm(nm, 8, cols),
                vm(nm, 8, cols),
                vm(nm + 2, 8, cols),
                vm(nm, 8, cols),
                vm(4, nm, cols),
                vm(nm, 8, cols),
                vm(SWEEPS, nm, 8, cols),
                vm(2, SWEEPS, nm, 2, cols),
                vm(2, SWEEPS, nm, cols),
                vm(2, nm, cols),
                vm(2, rows // 2, cols),
                vm(2, rows // 2, cols),
                vm(2, SWEEPS, rows, cols),
                vm(2, SWEEPS, nm, 2, cols),
                vm(nz, SWEEPS, nm, 8, cols),
                vm(2, 2, SWEEPS, 2, cols),
                vm(2, nz, SWEEPS, nm, cols),
                vm(2, nz, SWEEPS, 8, cols),
                vm(2, nm, cols),
                vm(nz, nm, 8, cols),
                pltpu.SemaphoreType.DMA((total_slots,)),
                pltpu.SemaphoreType.DMA((total_slots + rounds,)),
                pltpu.SemaphoreType.DMA((6,)),
                pltpu.SemaphoreType.DMA((4,)),
            ],
            compiler_params=pltpu.CompilerParams(
                collective_id=0, has_side_effects=True, vmem_limit_bytes=50 * 1024 * 1024
            ),
        )(field, source)

    spec = P("gx", "gy", "gz")
    return jax.shard_map(on_device, mesh=mesh, in_specs=(spec, spec), out_specs=spec, check_vma=False)
```

time: 28.5 us -> 25.7 us (0.902)
  Pallas kernels: 27 us -> 24.2 us
    pallas_call x1, Pallas kernels: 27 us -> 24.2 us  [on_device(): pl.pallas_call(functools.partial(kernel, sizes), out_shape=jax.ShapeDtype...]
where the time goes in v3:
time: 25.7 us; the launch traced here: 25.5 us
  Pallas kernels  24.2 us (94%)
  local copies, waits for them, and re-layouts  1.32 us (5%)
    pallas_call x1, Pallas kernels, on_device(): pl.pallas_call(functools.partial(kernel, sizes), out_shape=jax.ShapeDtype...  24.2 us
    unnamed x1, local copies, waits for them, and re-layouts  1.32 us

profile of v3, /device:TPU:1, one launch (start us, length us, event | category | flops | bytes accessed | tf_op | source)
XLA Modules:
  0.0 25.5 jit_solution(8271052528233523825)
XLA Ops:
  0.0 24.2 %shard_map.28 = f32[16,256,128]{2,1,0:T(8,128)S(1)} custom-call(f32[16,256,128]{2,1,0:T(8,128)} %f_hbm.1, f32[16,256,128]{2,1,0:T(8,128)} %s_hbm.1), custom_call_target="tpu_custom_call" | custom-call | tf_op jit(solution)/shard_map/pallas_call | solution.py:548
  24.2 1.3 %copy.4 = f32[16,256,128]{2,1,0:T(8,128)} copy(f32[16,256,128]{2,1,0:T(8,128)S(1)} %shard_map.28) | data formatting | bytes 4194304

commit v4 on v3

--- a/solution.py
+++ b/solution.py
@@ -125,11 +125,18 @@
         )
 
 
+    cross = lax.rem(gx, 2)
+    near = 1 - cross
+    sides = (near, cross)
+
+    def there(sx):
+        return jnp.where(sx == 1, gx < ngx - 1, gx > 0)
+
     def msg_x(sx, half, t):
         start = half * (rows // 2)
         return copy(
-            x1.at[edge_m[sx] + 1, pl.ds(PAD + start, rows // 2)], xg.at[1 - sx, t, pl.ds(start, rows // 2)],
-            {"gx": x_to[sx]}, "X", 2 * sx + half, t,
+            x1.at[sx * (nm - 1) + 1, pl.ds(PAD + start, rows // 2)], xg.at[1 - sx, t, pl.ds(start, rows // 2)],
+            {"gx": gx + 2 * sx - 1}, "X", 2 * sx + half, t,
         )
 
     def msg_y(sy, t):
@@ -150,11 +157,11 @@
 
     def msg_xz(sx, zd, t):
         return copy(
-            pk.at[t, edge_m[sx]], xzr.at[1 - sx, zd, t], {"gx": x_to[sx], "gz": z_to[zd]}, "XZ", nz * sx + zd, t
+            pk.at[t, sx * (nm - 1)], xzr.at[1 - sx, zd, t], {"gx": gx + 2 * sx - 1, "gz": z_to[zd]}, "XZ", nz * sx + zd, t
         )
 
     def msg_sx(sx):
-        return copy(sxs.at[sx], sxr.at[1 - sx], {"gx": x_to[sx]}, "SX", sx, 0)
+        return copy(sxs.at[sx], sxr.at[1 - sx], {"gx": gx + 2 * sx - 1}, "SX", sx, 0)
 
     def source_face(sx):
         even = s0[edge_m[sx] + 1, pl.ds(PAD, rows // 2, stride=2), :]
@@ -181,12 +188,10 @@
         for sy in range(2):
             msg_y(sy, t).start()
 
-    def send_x(half, t):
-        for sx in range(2):
-
-            @pl.when(has[sx])
-            def _():
-                msg_x(sx, half, t).start()
+    def send_x(sx, half, t):
+        @pl.when(there(sx))
+        def _():
+            msg_x(sx, half, t).start()
 
     def send_z(part, t):
         for zd in range(nz):
@@ -296,16 +301,17 @@
             for m in range(nm):
                 field_rows(m, (g,))
                 keep_rows(0, m, x1[m + 1, rows_of(g), :], sy)
-    near = [h.astype(jnp.int32) for h in has]
+    links = [h.astype(jnp.int32) for h in has]
     with jax.named_scope("barrier"):
-        pl.semaphore_wait(barrier, 2 + 3 * nz + (near[0] + near[1]) * (3 + nz))
+        pl.semaphore_wait(barrier, 2 + 3 * nz + (links[0] + links[1]) * (3 + nz))
     send_far(0)
     with jax.named_scope("field"):
         for part in range(2):
             load_field(part).wait()
             field_plane(edge_m[part])
-        for half in range(2):
-            send_x(half, 0)
+        for sx in (cross, near):
+            for half in range(2):
+                send_x(sx, half, 0)
     pack_edges(0)
     for part in range(2):
         with jax.named_scope("field"):
@@ -373,11 +379,12 @@
     hi_z = nz - 1
 
     def ghost_plane(sx, groups):
-        m = (-1, nm)[sx]
+        m = sx * (nm + 1) - 1
         v = eb[m + 1]
+        on = there(sx)
         for g in groups:
-            y = tile(0, m, g, edge_at(v, g), (1, -1)[sx])
-            x0[m + 1, rows_of(g), :] = jnp.where(has[sx], y, 0.0)
+            y = tile(0, m, g, edge_at(v, g), 1 - 2 * sx)
+            x0[m + 1, rows_of(g), :] = jnp.where(on, y, 0.0)
 
     def take_z(part, t):
         with jax.named_scope("waitz"):
@@ -387,6 +394,25 @@
             lo, hi = zr[0, t, m], zr[hi_z, t, m]
             qb[m + 1] = jnp.where(low_half, lo, hi)
             eb[m + 1] = swapped(lo, hi)
+
+    def take_x(sx, half, t):
+        at = sx * (nm + 1)
+        rs = pl.ds(half * (rows // 2), rows // 2)
+
+        @pl.when(there(sx))
+        def _():
+            if half == 0:
+                for zd in range(nz):
+                    msg_xz(1 - sx, zd, t).wait_recv()
+                lo, hi = xzr[sx, 0, t], xzr[sx, hi_z, t]
+                qb[at] = jnp.where(low_half, lo, hi)
+                eb[at] = swapped(lo, hi)
+                if t == 0:
+                    msg_sx(1 - sx).wait_recv()
+                    for row in range(2):
+                        s0[at, pl.ds(PAD + row, rows // 2, stride=2), :] = sxr[sx]
+            msg_x(1 - sx, half, t).wait_recv()
+            x1[at, pl.ds(PAD + half * (rows // 2), rows // 2), :] = xg[sx, t, rs, :]
 
     z_early = lax.rem(gx, 2) == 1
 
@@ -431,36 +457,24 @@
         for part in range(2):
             take_z(part, t)
 
+        with jax.named_scope("waitxn"):
+            for half in range(2):
+                take_x(near, half, t)
+        with jax.named_scope("P2n"):
+            ghost_plane(near, inner)
+            red_plane(near * (nm - 1), inner)
+
         @pl.when(z_early)
         def _():
             close_inner(t)
 
         for half in range(2):
-            start = half * (rows // 2)
             groups = (inner[: ng // 2 - 2], inner[ng // 2 - 2 :])[half]
             with jax.named_scope("waitx"):
-                for sx in range(2):
-                    at = (0, nm + 1)[sx]
-
-                    @pl.when(has[sx])
-                    def _():
-                        if half == 0:
-                            for zd in range(nz):
-                                msg_xz(1 - sx, zd, t).wait_recv()
-                            lo, hi = xzr[sx, 0, t], xzr[sx, hi_z, t]
-                            qb[at] = jnp.where(low_half, lo, hi)
-                            eb[at] = swapped(lo, hi)
-                            if t == 0:
-                                msg_sx(1 - sx).wait_recv()
-                                for row in range(2):
-                                    s0[at, pl.ds(PAD + row, rows // 2, stride=2), :] = sxr[sx]
-                        msg_x(1 - sx, half, t).wait_recv()
-                        x1[at, pl.ds(PAD + start, rows // 2), :] = xg[sx, t, pl.ds(start, rows // 2), :]
-
+                take_x(cross, half, t)
             with jax.named_scope("P2"):
-                for sx in range(2):
-                    ghost_plane(sx, groups)
-                    red_plane(edge_m[sx], groups)
+                ghost_plane(cross, groups)
+                red_plane(cross * (nm - 1), groups)
 
         @pl.when(jnp.logical_not(z_early))
         def _():
@@ -522,10 +536,13 @@
             for m in range(nm):
                 er[m] = swapped(rq[m], rq[m])
             for half, groups in enumerate((inner[: ng // 2 - 1], inner[ng // 2 - 1 :])):
-                for m in edge_m:
-                    black_plane(m, groups, final)
+                black_plane(cross * (nm - 1), groups, final)
                 if not final:
-                    send_x(half, t + 1)
+                    send_x(cross, half, t + 1)
+            black_plane(near * (nm - 1), inner, final)
+            if not final:
+                for half in range(2):
+                    send_x(near, half, t + 1)
         if not final:
             pack_edges(t + 1)
         for part in range(2):

time: 25.7 us -> 25.1 us (0.977)
  Pallas kernels: 24.2 us -> 23.6 us
    pallas_call x1, Pallas kernels: 24.2 us -> 23.6 us  [on_device(): pl.pallas_call(functools.partial(kernel, sizes), out_shape=jax.ShapeDtype...]
where the time goes in v4:
time: 25.1 us; the launch traced here: 24.9 us
  Pallas kernels  23.6 us (94%)
  local copies, waits for them, and re-layouts  1.32 us (5%)
    pallas_call x1, Pallas kernels, on_device(): pl.pallas_call(functools.partial(kernel, sizes), out_shape=jax.ShapeDtype...  23.6 us
    unnamed x1, local copies, waits for them, and re-layouts  1.32 us

profile of v4, /device:TPU:1, one launch (start us, length us, event | category | flops | bytes accessed | tf_op | source)
XLA Modules:
  0.0 24.9 jit_solution(3816502423320695972)
XLA Ops:
  0.0 23.6 %shard_map.28 = f32[16,256,128]{2,1,0:T(8,128)S(1)} custom-call(f32[16,256,128]{2,1,0:T(8,128)} %f_hbm.1, f32[16,256,128]{2,1,0:T(8,128)} %s_hbm.1), custom_call_target="tpu_custom_call" | custom-call | tf_op jit(solution)/shard_map/pallas_call | solution.py:565
  23.6 1.3 %copy.4 = f32[16,256,128]{2,1,0:T(8,128)} copy(f32[16,256,128]{2,1,0:T(8,128)S(1)} %shard_map.28) | data formatting | bytes 4194304

commit v5 on v4

--- a/solution.py
+++ b/solution.py
@@ -25,7 +25,7 @@
 
 
 def kernel(
-    sizes, f_hbm, s_hbm, ov, fv, sv, x0, x1, s0, s1, eb, er, rq, qb, sq, yzb, sqs,
+    sizes, f_hbm, s_hbm, x0, s1, er, fv, sv, x1, s0, eb, rq, qb, sq, yzb, sqs,
     pk, jb, yzs, sys_, sxs, sxr, xg, jr, zr, xyr, yzr, xzr, syr, szr, send, recv, fsem, ssem,
 ):
     ngx, ngy, ngz = sizes
@@ -358,19 +358,13 @@
         for g in groups:
             x0[m + 1, rows_of(g), :] = tile(0, m, g, edge_at(v, g), side)
 
-    def put(m, g, y, final):
-        if final:
-            red = x0[m + 1, rows_of(g), :]
-            rs = pl.ds(8 * g, 8)
-            ov[2 * m, rs, :] = jnp.where(odd, y, red)
-            ov[2 * m + 1, rs, :] = jnp.where(odd, red, y)
-        else:
-            x1[m + 1, rows_of(g), :] = y
-
-    def black_plane(m, groups, final):
+    def put(m, g, y):
+        x1[m + 1, rows_of(g), :] = y
+
+    def black_plane(m, groups):
         v = er[m]
         for g in groups:
-            put(m, g, tile(1, m, g, edge_at(v, g)), final)
+            put(m, g, tile(1, m, g, edge_at(v, g)))
 
     def swapped(lo, hi):
         return jnp.where(pos1, roll(hi, -1), roll(lo, 1))
@@ -522,34 +516,76 @@
                 total = rq[m] + jnp.where(no_up, jnp.broadcast_to(yzb[0, pl.ds(m, 1), :], (8, cols)), 0.0)
                 total = total + jnp.where(no_down, jnp.broadcast_to(yzb[1, pl.ds(m, 1), :], (8, cols)), 0.0)
                 rq[m] = total * jnp.float32(SIXTH)
+            if final:
+                for m in range(nm):
+                    er[m] = swapped(rq[m], rq[m])
+                break
             for m in range(nm):
                 red = rq[m]
                 for sy, g in ((0, 0), (1, ng - 1)):
                     y = tile(1, m, g, roll(red, -(4 * g + 1)), None, roll(red, -(4 * g + 3)))
-                    put(m, g, y, final)
-                    if not final:
-                        keep_rows(t + 1, m, y, sy)
-
-        if not final:
-            send_far(t + 1)
+                    put(m, g, y)
+                    keep_rows(t + 1, m, y, sy)
+
+        send_far(t + 1)
         with jax.named_scope("P4"):
             for m in range(nm):
                 er[m] = swapped(rq[m], rq[m])
             for half, groups in enumerate((inner[: ng // 2 - 1], inner[ng // 2 - 1 :])):
-                black_plane(cross * (nm - 1), groups, final)
-                if not final:
-                    send_x(cross, half, t + 1)
-            black_plane(near * (nm - 1), inner, final)
-            if not final:
-                for half in range(2):
-                    send_x(near, half, t + 1)
-        if not final:
-            pack_edges(t + 1)
+                black_plane(cross * (nm - 1), groups)
+                send_x(cross, half, t + 1)
+            black_plane(near * (nm - 1), inner)
+            for half in range(2):
+                send_x(near, half, t + 1)
+        pack_edges(t + 1)
         for part in range(2):
             with jax.named_scope("P5"):
-                several(*middle[part], 3, lambda m: black_plane(m, inner, final))
-            if not final:
-                pack(part, t + 1)
+                several(*middle[part], 3, lambda m: black_plane(m, inner))
+            pack(part, t + 1)
+
+
+def finish(x0, s1, er, o_hbm, ov, sem):
+    planes, rows, cols = ov.shape
+    nm, ng, step = planes // 2, rows // 8, 2
+    sub = lax.broadcasted_iota(jnp.int32, (8, cols), 0)
+    lane = lax.broadcasted_iota(jnp.int32, (8, cols), 1)
+    odd = lax.rem(sub + lane, 2) == 1
+    first, final_lane = lane == 0, lane == cols - 1
+
+    def out(i):
+        at = pl.ds(2 * step * i, 2 * step)
+        return pltpu.make_async_copy(ov.at[at], o_hbm.at[at], sem.at[i])
+
+    def plane(m):
+        v = er[m]
+        for g in range(ng):
+            rs = pl.ds(PAD + 8 * g, 8)
+            here = x0[m + 1, rs, :]
+            beside = jnp.where(odd, x0[m, rs, :], x0[m + 2, rs, :])
+            edge = pltpu.roll(v, (2 * cols - (4 * g + 2)) % cols, 1)
+            total = (s1[m, rs, :] + here) + (beside + x0[m + 1, pl.ds(PAD + 8 * g - 1, 8), :])
+            total = total + x0[m + 1, pl.ds(PAD + 8 * g + 1, 8), :]
+            total = total + jnp.where(first, edge, pltpu.roll(here, 1, 1))
+            total = total + jnp.where(final_lane, edge, pltpu.roll(here, cols - 1, 1))
+            y = total * jnp.float32(SIXTH)
+            to = pl.ds(8 * g, 8)
+            ov[2 * m, to, :] = jnp.where(odd, y, here)
+            ov[2 * m + 1, to, :] = jnp.where(odd, here, y)
+
+    def body(i, carry):
+        for k in range(step):
+            plane(step * i + k)
+
+        @pl.when(i > 0)
+        def _():
+            out(i - 1).start()
+
+        return carry
+
+    lax.fori_loop(0, nm // step, body, 0)
+    out(nm // step - 1).start()
+    for i in range(nm // step):
+        out(i).wait()
 
 
 def solution(mesh):
@@ -562,20 +598,20 @@
         _, rounds, total_slots = slots(nz)
         f32 = jnp.float32
         vm = lambda *shape: pltpu.VMEM(shape, f32)
-        return pl.pallas_call(
+        shape = lambda *dims: jax.ShapeDtypeStruct(dims, f32)
+        in_vmem = pl.BlockSpec(memory_space=pltpu.VMEM)
+        wide = rows + 2 * PAD
+        kept = pl.pallas_call(
             functools.partial(kernel, sizes),
-            out_shape=jax.ShapeDtypeStruct(field.shape, f32),
+            out_shape=[shape(nm + 2, wide, cols), shape(nm, wide, cols), shape(nm, 8, cols)],
             in_specs=[pl.BlockSpec(memory_space=pltpu.HBM)] * 2,
-            out_specs=pl.BlockSpec(memory_space=pltpu.VMEM),
+            out_specs=[in_vmem] * 3,
             scratch_shapes=[
                 vm(*field.shape),
                 vm(*field.shape),
-                vm(nm + 2, rows + 2 * PAD, cols),
-                vm(nm + 2, rows + 2 * PAD, cols),
-                vm(nm + 2, rows + 2 * PAD, cols),
-                vm(nm, rows + 2 * PAD, cols),
+                vm(nm + 2, wide, cols),
+                vm(nm + 2, wide, cols),
                 vm(nm + 2, 8, cols),
-                vm(nm, 8, cols),
                 vm(nm, 8, cols),
                 vm(nm + 2, 8, cols),
                 vm(nm, 8, cols),
@@ -601,9 +637,17 @@
                 pltpu.SemaphoreType.DMA((4,)),
             ],
             compiler_params=pltpu.CompilerParams(
-                collective_id=0, has_side_effects=True, vmem_limit_bytes=50 * 1024 * 1024
+                collective_id=0, has_side_effects=True, vmem_limit_bytes=51 * 1024 * 1024
             ),
         )(field, source)
+        return pl.pallas_call(
+            finish,
+            out_shape=shape(planes, rows, cols),
+            in_specs=[in_vmem] * 3,
+            out_specs=pl.BlockSpec(memory_space=pltpu.HBM),
+            scratch_shapes=[vm(planes, rows, cols), pltpu.SemaphoreType.DMA((nm // 2,))],
+            compiler_params=pltpu.CompilerParams(vmem_limit_bytes=12 * 1024 * 1024),
+        )(*kept)
 
     spec = P("gx", "gy", "gz")
     return jax.shard_map(on_device, mesh=mesh, in_specs=(spec, spec), out_specs=spec, check_vma=False)

time: 25.1 us -> 25 us (level)
  local copies, waits for them, and re-layouts: 1.32 us -> 0 us
  Pallas kernels: 23.6 us -> 24.8 us
    unnamed x1 -> x0, local copies, waits for them, and re-layouts: 1.32 us -> none
    pallas_call x1 -> x2, Pallas kernels: 23.6 us -> 24.8 us  [the longest x1 22.7 us: on_device(): pl.pallas_call(functools.partial(kernel, sizes), out_shape=[shape(nm + 2,...]
where the time goes in v5:
time: 25 us; the launch traced here: 24.8 us
  Pallas kernels  24.8 us (99%)
    pallas_call x1, Pallas kernels, on_device(): pl.pallas_call(functools.partial(kernel, sizes), out_shape=[shape(nm + 2,...  22.7 us
    pallas_call x1, Pallas kernels, on_device(): pl.pallas_call(finish, out_shape=shape(planes, rows, cols), in_specs=[in_...  2.09 us

profile of v5, /device:TPU:1, one launch (start us, length us, event | category | flops | bytes accessed | tf_op | source)
XLA Modules:
  0.0 24.8 jit_solution(11888010948858683123)
XLA Ops:
  0.0 22.7 %shard_map.28 = (f32[10,288,128]{2,1,0:T(8,128)S(1)}, f32[8,288,128]{2,1,0:T(8,128)S(1)}, f32[8,8,128]{2,1,0:T(8,128)S(1)}) custom-call(f32[16,256,128]{2,1,0:T(8,128)} %f_hbm.1, f32[16,256,128]{2,1,0:T(8,128)} %s_hbm.1), custom_call_target="tpu_custom_call" | custom-call | tf_op jit(solution)/shard_map/pallas_call | solution.py:604
  22.7 2.1 %shard_map.29 = f32[16,256,128]{2,1,0:T(8,128)} custom-call(f32[10,288,128]{2,1,0:T(8,128)S(1)} %get-tuple-element.8.x0, f32[8,288,128]{2,1,0:T(8,128)S(1)} %get-tuple-element.9.s1, f32[8,8,128]{2,1,0:T(8,128)S(1)} %get-tuple-element.10.er), custom_call_target="tpu_custom_call" | custom-call | tf_op jit(solution)/shard_map/pallas_call | solution.py:643
